TPU v7x, 256 devices: a whole 4x4x8 slice. The times are simulated.
256 devices in a mesh: slab: 32 (over x, y, core), probe: 8 (over z).
Axes of the slice: x: 4, y: 4, z: 8, core: 2. Of those that a mesh axis runs over, the one named last changes fastest.
Arguments:
- probes: float32 [16, 3, 64, 128, 128], P('probe', None, 'slab'), may hold values from -50 to 50
- earlier: float32 [16, 3, 64, 128, 128], P(None, None, 'slab', 'probe'), may hold values from -16 to 16
- modulus: float32 [64, 128, 128], P('slab'), may hold values from 0.5 to 2
- tangent: float32 [6, 64, 128, 128], P(None, 'slab'), may hold values from -0.3 to 2, as said below
Outputs:
- basis: float32 [16, 3, 64, 128, 128], P('probe', None, 'slab')
- correlation: float32 [16, 16], replicated
Inputs may be any that keep to these rules, and one draw needn't show every extreme that they name: `tangent`: entries 0 to 2 lie in 1 to 2, entries 3 to 5 in -0.3 to 0.3.
All inputs are finite; a program needn't handle non-finite values.
Results may differ from a plain program's by a relative error of at most 0.00014.
Values sent between devices are 32-bit elements; how exact they have to be, the bound alone decides.
No kernel may reach another device: no remote copies, remote signals or barrier semaphores. Data moves between devices by JAX's collectives and lax.ppermute only.
A program may use at most 64 MiB of HBM per device.

v0:
```python
import functools
import math

import jax
import jax.numpy as jnp
from jax import lax
from jax.experimental import pallas as pl
from jax.experimental.pallas import tpu as pltpu
from jax.sharding import Mesh
from jax.sharding import PartitionSpec as P

STRIP = 16
PART = 0.05 / 16.0


def rows_at(ref, lead, start, shift, height):
    first = start + shift
    if first < 0:
        block = pltpu.roll(ref[lead + (pl.ds(0, STRIP), slice(None))], 1, 0)
        row = lax.broadcasted_iota(jnp.int32, block.shape, 0)
        return jnp.where(row == 0, 0.0, block)
    if first + STRIP > height:
        block = pltpu.roll(ref[lead + (pl.ds(height - STRIP, STRIP), slice(None))], STRIP - 1, 0)
        row = lax.broadcasted_iota(jnp.int32, block.shape, 0)
        return jnp.where(row == STRIP - 1, 0.0, block)
    return ref[lead + (pl.ds(first, STRIP), slice(None))]


def across(block):
    breadth = block.shape[1]
    lane = lax.broadcasted_iota(jnp.int32, block.shape, 1)
    left = jnp.where(lane == 0, 0.0, pltpu.roll(block, 1, 1))
    right = jnp.where(lane == breadth - 1, 0.0, pltpu.roll(block, breadth - 1, 1))
    return left + right


def outer_sum(mid, above, below):
    tall = (mid + mid) + (above + below)
    both = tall + mid
    return across(tall) + (both + both)


def full_sum(mid, pair_y, side, side_y):
    near = pair_y + side
    six = 6.0 * mid
    inner = (near + near) + (six + side_y)
    rest = inner + (near - six)
    return across(inner) + (rest + rest)


def combine(diag, off, fields):
    a, b, c = fields
    return (
        diag[0] * a + off[0] * b + off[1] * c,
        off[0] * a + diag[1] * b + off[2] * c,
        off[1] * a + off[2] * b + diag[2] * c,
    )


def lift_kernel(place, probes_far, modulus_far, out, sems):
    count = probes_far.shape[0]
    core = place[0]
    copies = [
        pltpu.make_async_copy(probes_far.at[k, :, core], out.at[pl.ds(3 * k, 3)], sems.at[k]) for k in range(count)
    ]
    copies.append(pltpu.make_async_copy(modulus_far.at[pl.ds(core, 1)], out.at[pl.ds(3 * count, 1)], sems.at[count]))
    for copy in copies:
        copy.start()
    for copy in copies:
        copy.wait()


def partial_kernel(place, probes_far, modulus_far, tangent_far, far, near, probes, modulus, tangent, prod, sems):
    count = probes.shape[0]
    height = probes.shape[3]
    core = place[0]
    copies = []
    for z, plane in ((0, core), (1, 1 - core)):
        triples = (
            (modulus_far.at[pl.ds(plane, 1)], modulus.at[pl.ds(z, 1)]),
            (probes_far.at[:, :, pl.ds(plane, 1)], probes.at[:, :, pl.ds(z, 1)]),
            (tangent_far.at[:, pl.ds(plane, 1)], tangent.at[:, pl.ds(z, 1)]),
        )
        copies.append([pltpu.make_async_copy(src, dst, sems.at[z, n]) for n, (src, dst) in enumerate(triples)])
    for n in range(3):
        copies[0][n].start()
        copies[1][n].start()
    for n in range(2):
        copies[0][n].wait()
        copies[1][n].wait()
    for z in range(2):
        for k in range(count):
            for i in range(3):
                prod[z * 3 * count + 3 * k + i] = probes[k, i, z] * modulus[z]
    copies[0][2].wait()
    copies[1][2].wait()
    for z, out in ((0, far), (1, near)):
        other = 1 - z
        for s in range(0, height, STRIP):
            here = pl.ds(s, STRIP)

            def mod(plane, shift):
                return rows_at(modulus, (plane,), s, shift, height)

            m = mod(z, 0)
            side = mod(other, 0)
            neighbours = full_sum(m, mod(z, -1) + mod(z, 1), side, mod(other, -1) + mod(other, 1))
            common = (3.4 / 16.0) * m + PART * neighbours - 1.0
            diag = [common + 0.125 * tangent[i, z, here, :] for i in range(3)]
            off = [0.125 * tangent[3 + i, z, here, :] for i in range(3)]
            scaled = PART * m
            if z:
                out[6 * count, here, :] = m
            for k in range(count):
                values = [probes[k, i, z, here, :] for i in range(3)]
                mixed = combine(diag, off, values)
                for i in range(3):
                    def val(plane, shift):
                        return rows_at(probes, (k, i, plane), s, shift, height)

                    def pro(plane, shift):
                        return rows_at(prod, (plane * 3 * count + 3 * k + i,), s, shift, height)

                    first = full_sum(values[i], val(z, -1) + val(z, 1), val(other, 0), val(other, -1) + val(other, 1))
                    second = full_sum(pro(z, 0), pro(z, -1) + pro(z, 1), pro(other, 0), pro(other, -1) + pro(other, 1))
                    if z:
                        out[3 * k + i, here, :] = values[i]
                    out[3 * count * z + 3 * k + i, here, :] = mixed[i] - scaled * first - PART * second


def filter_kernel(place, lo, lo_part, down, down_part, up, hi, tangent_far, out, tangent, once, prod, sums, products, prior, sems):
    planes = (lo, down, up, hi)
    core = place[0]
    parts = (lo_part, down_part, up, hi)
    copies = [
        pltpu.make_async_copy(tangent_far.at[:, pl.ds(plane, 1)], tangent.at[:, pl.ds(z, 1)], sems.at[z])
        for z, plane in ((0, core), (1, 1 - core))
    ]
    for copy in copies:
        copy.start()
    total = lo.shape[0] - 1
    count = total // 3
    height = lo.shape[1]
    blocks = height // STRIP
    last = (total, total, 2 * total, 2 * total)
    start = (0, 0, total, total)
    mods = [planes[z][last[z]] for z in range(4)]
    for z in range(4):
        for n in range(total):
            prior[z * total + n] = planes[z][n] * mods[z]
    for source, target in ((0, 1), (1, 0), (2, 3), (3, 2)):
        src = planes[source]
        dst = planes[target]
        for s in range(0, height, STRIP):
            here = pl.ds(s, STRIP)

            def at(ref, n, shift):
                return rows_at(ref, (n,), s, shift, height)

            m = dst[last[target], here, :]
            weight = PART * outer_sum(*(at(src, last[source], d) for d in (0, -1, 1)))
            scaled = PART * m
            for n in range(total):
                first = outer_sum(at(src, n, 0), at(src, n, -1), at(src, n, 1))
                j = source * total + n
                second = outer_sum(at(prior, j, 0), at(prior, j, -1), at(prior, j, 1))
                value = parts[target][start[target] + n, here, :] + weight * dst[n, here, :] - scaled * first - PART * second
                if target in (0, 3):
                    value = jnp.where(m > 0.0, value, 0.0)
                once[target * total + n, here, :] = value
                prod[target * total + n, here, :] = value * m
    for z in (1, 2):
        for n in range(total):
            sums[(z - 1) * total + n] = once[(z - 1) * total + n] + once[(z + 1) * total + n]
            products[(z - 1) * total + n] = prod[(z - 1) * total + n] + prod[(z + 1) * total + n]
    for copy in copies:
        copy.wait()
    for z, depth in ((1, core), (2, 1 - core)):
        plane = planes[z]
        for s in range(0, height, STRIP):
            here = pl.ds(s, STRIP)

            def at(ref, n, shift):
                return rows_at(ref, (n,), s, shift, height)

            def mod(p, shift):
                return rows_at(planes[p], (last[p],), s, shift, height)

            m = mod(z, 0)
            side = [mod(z - 1, d) + mod(z + 1, d) for d in (-1, 0, 1)]
            neighbours = full_sum(m, mod(z, -1) + mod(z, 1), side[1], side[0] + side[2])
            common = (6.8 / 16.0) * m + (2.0 * PART) * neighbours - 2.0
            diag = [common + 0.25 * tangent[i, z - 1, here, :] for i in range(3)]
            off = [0.25 * tangent[3 + i, z - 1, here, :] for i in range(3)]
            scaled = (2.0 * PART) * m
            turn = lax.rem(s // STRIP + blocks - place[1], blocks)
            for k in range(count):
                base = z * total + 3 * k
                mixed = combine(diag, off, [once[base + i, here, :] for i in range(3)])
                for i in range(3):
                    n = base + i
                    j = n - total
                    first = full_sum(at(once, n, 0), at(once, n, -1) + at(once, n, 1), at(sums, j, 0), at(sums, j, -1) + at(sums, j, 1))
                    second = full_sum(at(prod, n, 0), at(prod, n, -1) + at(prod, n, 1), at(products, j, 0), at(products, j, -1) + at(products, j, 1))
                    value = mixed[i] - scaled * first - (2.0 * PART) * second - plane[3 * k + i, here, :]
                    out[turn, k, i, depth] = value


def split(block):
    high = block.astype(jnp.bfloat16).astype(jnp.float32)
    rest = block - high
    middle = rest.astype(jnp.bfloat16).astype(jnp.float32)
    return high, middle, rest - middle


def piled(block):
    parts = list(split(block))
    if block.shape[0] % 16:
        parts.append(jnp.zeros_like(block))
    return jnp.concatenate(parts, axis=0).astype(jnp.bfloat16)


def folded(block, count, start, axis):
    pieces = [lax.slice_in_dim(block, start + n * count, start + (n + 1) * count, axis=axis) for n in range(3)]
    return (pieces[0] + pieces[1]) + pieces[2]


WIDE = 8


def gram_kernel(place, *refs, pieces, alone):
    stack, out, tall = refs[-3:]
    chunks = refs[: len(pieces)]
    earlier = refs[len(pieces) : -3]
    length = stack.shape[0]
    count = tall.shape[0] // length
    for chunk, (turn, first) in zip(chunks, pieces):
        each = chunk.shape[0]
        base = first
        if not alone:
            source = place[1] - turn
            base = first + 2 * jnp.where(source < 0, source + count // 2, source)
        for j in range(each):
            tall[pl.ds(base + j, length, stride=count), :] = chunk[j]

    def step(r, gram):
        rows = []
        for h in range(WIDE):
            here = WIDE * r + h
            pile = piled(tall[pl.ds(here * count, count), :])
            stack[here] = pile
            rows.append(pile)
        own = jnp.concatenate(rows, axis=1)
        others = [jnp.concatenate([e[WIDE * r + h] for h in range(WIDE)], axis=1) for e in earlier]
        every = jnp.concatenate(others + [own], axis=0)
        return gram + lax.dot_general(own, every, (((1,), (1,)), ((), ())), preferred_element_type=jnp.float32)

    width = 3 * count * (1 + len(earlier))
    gram = lax.fori_loop(0, length // WIDE, step, jnp.zeros((3 * count, width), jnp.float32), unroll=2)
    gram = folded(gram, count, 0, 0)
    found = [folded(gram, count, 3 * count * n, 1) for n in range(1 + len(earlier))]
    if alone:
        found.append(jnp.zeros((count, count), jnp.float32))
    out[...] = jnp.concatenate(found, axis=1)


def pack_kernel(first, second, out):
    gram = jnp.concatenate([first[...], second[...]], axis=0)
    packed = jnp.concatenate([gram[8 * q : 8 * q + 8] for q in range(gram.shape[0] // 8)], axis=1)
    for n in range(out.shape[0]):
        out[n] = packed


def finish_kernel(place, copies, first, second, scale, out, correlation):
    length = first.shape[0]
    kept = first.shape[1] // 3
    made = second.shape[1] // 3
    total = kept + made
    summed = copies[0]
    for n in range(1, copies.shape[0]):
        summed = summed + copies[n]
    gram = jnp.concatenate([summed[:, total * q : total * q + total] for q in range(total // 8)], axis=0)
    row = lax.broadcasted_iota(jnp.int32, (total, total), 0)
    column = lax.broadcasted_iota(jnp.int32, (total, total), 1)
    unit = jnp.where(row == column, 1.0, 0.0)
    strict = jnp.where(row > column, gram, 0.0)
    mirrored = lax.dot_general(strict, unit, (((0,), (0,)), ((), ())), precision=lax.Precision.HIGHEST)
    gram = jnp.where(row >= column, gram, mirrored)
    work = jnp.concatenate([gram, unit, jnp.zeros((total, 128 - 2 * total), jnp.float32)], axis=1)
    slot = lax.broadcasted_iota(jnp.int32, (total, 1), 0)
    pivots = jnp.zeros((total, 1), jnp.float32)
    factor = scale[0]
    for k in range(total):
        if k == kept:
            correlation[...] = -factor * work[kept:, total : total + kept]
        pivot = work[k : k + 1, k : k + 1]
        ratio = jnp.where(slot > k, work[:, k : k + 1] / pivot, 0.0)
        pivots = jnp.where(slot == k, pivot, pivots)
        work = work - ratio * work[k : k + 1, :]
    weights = factor * work[kept:, total : 2 * total] * lax.rsqrt(pivots[kept:])
    there = lax.broadcasted_iota(jnp.int32, (made, made), 0)
    source = lax.broadcasted_iota(jnp.int32, (made, made), 1)
    moved = there + 2 * place[1]
    turn = jnp.where(jnp.where(moved >= made, moved - made, moved) == source, 1.0, 0.0)
    weights = jnp.dot(turn, weights, precision=lax.Precision.HIGHEST)
    lines = []
    for part in split(weights):
        lines.append(jnp.concatenate([part[:, :kept]] * 3 + [part[:, kept:]] * 3, axis=1))
    left = jnp.concatenate(lines, axis=0).astype(jnp.bfloat16)
    for r in range(0, length, 2):
        sides = [jnp.concatenate([first[r + h], second[r + h]], axis=0) for h in range(2)]
        both = jnp.concatenate(sides, axis=1)
        wide_rows = lax.dot_general(left, both, (((1,), (0,)), ((), ())), preferred_element_type=jnp.float32)
        rows = (wide_rows[:made] + wide_rows[made : 2 * made]) + wide_rows[2 * made :]
        for h in range(2):
            out[pl.ds(r + h, made, stride=length), :] = rows[:, 128 * h : 128 * h + 128]


def out_turns(blocks):
    half = (len(blocks) - 1) // 2
    listed = []
    for n, block in enumerate(blocks):
        turn = n if n <= half else n - 1
        listed.append((block, turn, blocks[half].shape[0] if n == half + 1 else 0))
    return listed


def spread_kernel(place, *refs):
    blocks, out, sems = refs[:-2], refs[-2], refs[-1]
    turns = len(blocks) - 1
    copies = []
    for n, (block, k, first) in enumerate(out_turns(blocks)):
        source = lax.rem(place[1] + turns - k, turns)
        target = out.at[pl.ds(first, block.shape[0]), :, :, pl.ds(source * STRIP, STRIP), :]
        copies.append(pltpu.make_async_copy(block, target, sems.at[n]))
    for copy in copies:
        copy.start()
    for copy in copies:
        copy.wait()


VM = pl.BlockSpec(memory_space=pltpu.VMEM)
SM = pl.BlockSpec(memory_space=pltpu.SMEM)
FAR = pl.BlockSpec(memory_space=pltpu.HBM)


def near_chip(*arrays):
    return tuple(pltpu.with_memory_space_constraint(a, pltpu.VMEM) for a in arrays)


def in_far(*arrays):
    return tuple(pltpu.with_memory_space_constraint(a, pltpu.HBM) for a in arrays)


def lift_call(place, probes, modulus):
    count, _, _, height, breadth = probes.shape
    return pl.pallas_call(
        lift_kernel,
        out_shape=pltpu.VMEM((3 * count + 1, height, breadth), jnp.float32),
        in_specs=[SM, FAR, FAR],
        out_specs=VM,
        scratch_shapes=[pltpu.SemaphoreType.DMA((count + 1,))],
        compiler_params=pltpu.CompilerParams(vmem_limit_bytes=1 << 20),
        name="lift",
    )(place, *in_far(probes, modulus))


def partial_call(place, probes, modulus, tangent):
    count, _, _, height, breadth = probes.shape
    plane = lambda n: pltpu.VMEM((n, height, breadth), jnp.float32)
    return pl.pallas_call(
        partial_kernel,
        out_shape=(plane(3 * count), plane(6 * count + 1)),
        in_specs=[SM] + [FAR] * 3,
        out_specs=(VM, VM),
        scratch_shapes=[pltpu.VMEM(a.shape, jnp.float32) for a in (probes, modulus, tangent)]
        + [plane(6 * count), pltpu.SemaphoreType.DMA((2, 3))],
        compiler_params=pltpu.CompilerParams(vmem_limit_bytes=12 << 20),
        name="partial",
    )(place, *in_far(probes, modulus, tangent))


def filter_call(place, packs, tangent):
    packed, height, breadth = packs[0].shape
    total = packed - 1
    plane = lambda n: pltpu.VMEM((n, height, breadth), jnp.float32)
    return pl.pallas_call(
        filter_kernel,
        out_shape=pltpu.VMEM((height // STRIP, total // 3, 3, 2, STRIP, breadth), jnp.float32),
        in_specs=[SM] + [VM] * len(packs) + [FAR],
        out_specs=VM,
        scratch_shapes=[pltpu.VMEM(tangent.shape, jnp.float32), plane(4 * total), plane(4 * total)]
        + [plane(2 * total), plane(2 * total), plane(4 * total), pltpu.SemaphoreType.DMA((2,))],
        compiler_params=pltpu.CompilerParams(vmem_limit_bytes=16 << 20),
        name="filter",
    )(place, *near_chip(*packs), *in_far(tangent))


def gram_call(place, chunks, pieces, earlier=()):
    alone = not earlier
    length, breadth = chunks[0].shape[1:]
    count = sum(c.shape[0] for c in chunks)
    return pl.pallas_call(
        functools.partial(gram_kernel, pieces=pieces, alone=alone),
        out_shape=(
            pltpu.VMEM((length, 3 * count, breadth), jnp.bfloat16),
            pltpu.VMEM((count, 2 * count), jnp.float32),
        ),
        in_specs=[SM] + [VM] * (len(chunks) + len(earlier)),
        out_specs=(VM, VM),
        scratch_shapes=[pltpu.VMEM((length * count, breadth), jnp.float32)],
        compiler_params=pltpu.CompilerParams(vmem_limit_bytes=8 << 20),
        name="gram",
    )(place, *near_chip(*chunks, *earlier))


def pack_call(grams, copies):
    total = grams[0].shape[1]
    return pl.pallas_call(
        pack_kernel,
        out_shape=pltpu.VMEM((copies, 8, total * total // 8), jnp.float32),
        in_specs=[VM] * 2,
        out_specs=VM,
        compiler_params=pltpu.CompilerParams(vmem_limit_bytes=4 << 20),
        name="pack",
    )(*near_chip(*grams))


def finish_call(place, copies, stacks, scale):
    length, _, breadth = stacks[0].shape
    return pl.pallas_call(
        finish_kernel,
        out_shape=(
            pltpu.VMEM((16 * length, breadth), jnp.float32),
            jax.ShapeDtypeStruct((16, 16), jnp.float32),
        ),
        in_specs=[SM] + [VM] * 3 + [SM],
        out_specs=(VM, VM),
        compiler_params=pltpu.CompilerParams(vmem_limit_bytes=8 << 20),
        name="finish",
    )(place, *near_chip(copies, *stacks), scale)


def spread_call(place, blocks):
    count, parts, depth, strip, breadth = blocks[0].shape
    return pl.pallas_call(
        spread_kernel,
        out_shape=jax.ShapeDtypeStruct((count, parts, depth, strip * (len(blocks) - 1), breadth), jnp.float32),
        in_specs=[SM] + [VM] * len(blocks),
        out_specs=FAR,
        scratch_shapes=[pltpu.SemaphoreType.DMA((len(blocks),))],
        compiler_params=pltpu.CompilerParams(vmem_limit_bytes=8 << 20),
        name="spread",
    )(place, *near_chip(*blocks))


def shift(block, by, columns):
    return lax.ppermute(block, "probe", [(j, (j + by) % columns) for j in range(columns)])


def exchange(parts, columns):
    half = columns // 2
    cut = parts[half].shape[0] // 2
    got = [parts[0]] + [None] * (columns - 1)
    ahead = shift(parts[half][:cut], half, columns)
    back = shift(parts[half][cut:], -(half // 2), columns)
    for k in range(1, columns):
        if k != half:
            got[k] = shift(parts[k], k, columns)
    back = shift(back, half // 2 - half, columns)
    return got[:half] + [ahead, back] + got[half + 1 :]


def body(probes, earlier, modulus, tangent, slabs, columns, scale):
    kept = earlier.shape[0]
    breadth = earlier.shape[-1]
    length = math.prod(earlier.shape[1:-1])
    place = jnp.stack([lax.axis_index("core"), lax.axis_index("probe")]).astype(jnp.int32)
    places = ("x", "y", "core")
    outer = [(i, i + 1) for i in range(1, slabs - 1, 2)] + [(i, i - 1) for i in range(2, slabs, 2)]
    raw = lift_call(place, probes, modulus)
    got_raw = lax.ppermute(raw, places, outer)
    far, near = partial_call(place, probes, modulus, tangent)
    got_far = lax.ppermute(far, places, outer)
    got_near = lax.ppermute(near, "core", [(0, 1), (1, 0)])
    first, first_gram = gram_call(place, [earlier.reshape(kept, length, breadth)], ((0, 0),))
    filtered = filter_call(place, (got_raw, got_far, raw, far, near, got_near), tangent)
    got = exchange([filtered[k] for k in range(columns)], columns)
    half = columns // 2
    pieces = [(k, 0) for k in range(half + 1)] + [(half, 1)] + [(k, 0) for k in range(half + 1, columns)]
    flat = [g.reshape(g.shape[0], length, breadth) for g in got]
    second, second_gram = gram_call(place, flat, tuple(pieces), (first,))
    copies = pack_call((first_gram, second_gram), 2 * columns)
    copies = lax.all_to_all(copies, ("probe", "core"), 0, 0, tiled=True)
    copies = jnp.broadcast_to(jnp.sum(copies, axis=0, keepdims=True), (slabs // 2,) + copies.shape[1:])
    copies = lax.all_to_all(copies, ("x", "y"), 0, 0, tiled=True)
    rows, correlation = finish_call(place, copies, (first, second), scale.reshape(1))
    rows = rows.reshape((columns, 2) + earlier.shape[1:])
    got = exchange([rows[k] for k in range(columns)], columns)
    basis = spread_call(place, got)
    return (basis, correlation.T)


def solution(mesh):
    slabs = mesh.shape["slab"]
    columns = mesh.shape["probe"]
    side = math.isqrt(slabs // 2)
    wide = Mesh(mesh.devices.reshape(side, side, 2, columns), ("x", "y", "core", "probe"))
    slab = ("x", "y", "core")
    in_specs = (
        P("probe", None, slab, None, None),
        P(None, None, slab, "probe", None),
        P(slab, None, None),
        P(None, slab, None, None),
    )
    out_specs = (P("probe", None, slab, None, None), P())

    def step(probes, earlier, modulus, tangent):
        length = math.prod(probes.shape[1:])
        scale = jnp.sqrt(jnp.float32(length))
        inner = lambda *parts: body(*parts, slabs, columns, scale)
        return jax.shard_map(inner, mesh=wide, in_specs=in_specs, out_specs=out_specs, check_vma=False)(
            probes, earlier, modulus, tangent
        )

    return step
```

profile of v0, /device:TPU:2, one launch (start us, length us, event | category | flops | bytes accessed | tf_op | source)
XLA Modules:
  0.0 120.3 jit_solution(18291075691130622409)
XLA Ops:
  0.6 0.1 pad_add_fusion.place
  0.7 3.3 %partial.1 = (f32[6,128,128]{2,1,0:T(8,128)S(1)}, f32[13,128,128]{2,1,0:T(8,128)S(1)}) custom-call(s32[2]{0:T(128)S(1)} %pad_add_fusion.place, f32[2,3,2,128,128]{4,3,2,1,0:T(8,128)} %probes_far.3, f32[2,128,128]{2,1,0:T(8,128)} %modulus_far.3, f32[6,2,128,128]{3,2,1,0:T(8,128)} %tangent_far.3), custom_call_target="tpu_custom_call" | custom-call | tf_op jit(solution)/shard_map/partial/pallas_call | solution.py:371
  4.0 0.1 collective-permute-start.2
  4.1 1.6 %lift.1.down = f32[7,128,128]{2,1,0:T(8,128)S(1)} custom-call(s32[2]{0:T(128)S(1)} %pad_add_fusion.place, f32[2,3,2,128,128]{4,3,2,1,0:T(8,128)} %probes_far.3, f32[2,128,128]{2,1,0:T(8,128)} %modulus_far.3), custom_call_target="tpu_custom_call" | custom-call | tf_op jit(solution)/shard_map/lift/pallas_call | solution.py:357
  5.8 5.0 %collective-permute-start = (f32[7,128,128]{2,1,0:T(8,128)S(1)}, f32[7,128,128]{2,1,0:T(8,128)S(1)}, u32[]{:S(2)}, u32[]{:S(2)}) collective-permute-start(f32[7,128,128]{2,1,0:T(8,128)S(1)} %lift.1.down), channel_id=1, source_target_pairs={{8,16},{24,32},{40,48},{56,64},{72,80},{88,96},{104,112},{120,128}... | collective-permute-start | bytes 1376264 | tf_op jit(solution)/shard_map/ppermute | solution.py:482
  10.8 2.7 %collective-permute-start.1 = (f32[6,128,128]{2,1,0:T(8,128)S(1)}, f32[6,128,128]{2,1,0:T(8,128)S(1)}, u32[]{:S(2)}, u32[]{:S(2)}) collective-permute-start(f32[6,128,128]{2,1,0:T(8,128)S(1)} %get-tuple-element.11.down_part), channel_id=1, source_target_pairs={{8,16},{24,32},{40,48},{56,64},{72,80},{88,96},{104,112},{120,128}... | collective-permute-start | bytes 1179656 | tf_op jit(solution)/shard_map/ppermute | solution.py:484
  13.4 8.5 %collective-permute-done.1.lo_part = f32[6,128,128]{2,1,0:T(8,128)S(1)} collective-permute-done((f32[6,128,128]{2,1,0:T(8,128)S(1)}, f32[6,128,128]{2,1,0:T(8,128)S(1)}, u32[]{:S(2)}, u32[]{:S(2)}) %collective-permute-start.1) | collective-permute-done | bytes 393248 | tf_op jit(solution)/shard_map/ppermute | solution.py:484
  22.0 0.0 collective-permute-done.lo
  22.0 0.0 collective-permute-done.2.hi
  22.0 4.0 %filter.1 = f32[8,2,3,2,16,128]{5,4,3,2,1,0:T(8,128)S(1)} custom-call(s32[2]{0:T(128)S(1)} %pad_add_fusion.place, f32[7,128,128]{2,1,0:T(8,128)S(1)} %collective-permute-done.lo, f32[6,128,128]{2,1,0:T(8,128)S(1)} %collective-permute-done.1.lo_part, f32[7,128,128]{2,1,0:T(8,128)S(1)} %lift.1.down, f32[6,128,128]{2,1,0:T(8,128)S(1)} %get-tuple-element.11.down_part, ...), custom_call_target="tpu_custom_call" | custom-call | tf_op jit(solution)/shard_map/filter/pallas_call | solution.py:387
  25.9 0.0 copy-start
  26.0 6.8 %collective-permute-start.9 = (f32[2,3,2,16,128]{4,3,2,1,0:T(8,128)S(1)}, f32[2,3,2,16,128]{4,3,2,1,0:T(8,128)S(1)}, u32[]{:S(2)}, u32[]{:S(2)}) collective-permute-start(f32[2,3,2,16,128]{4,3,2,1,0:T(8,128)S(1)} %get-tuple-element.31), channel_id=1, source_target_pairs={{0,5},{1,6},{2,7},{3,0},{4,1},{5,2},{6,3},{7,4},{8,13},{9,14},{10,... | collective-permute-start | bytes 294920 | tf_op jit(solution)/shard_map/ppermute | solution.py:458
  32.8 0.6 collective-permute-start.7
  33.5 4.5 %collective-permute-start.6 = (f32[1,3,2,16,128]{4,3,2,1,0:T(8,128)S(1)}, f32[1,3,2,16,128]{4,3,2,1,0:T(8,128)S(1)}, u32[]{:S(2)}, u32[]{:S(2)}) collective-permute-start(f32[1,3,2,16,128]{4,3,2,1,0:T(8,128)S(1)} %get-tuple-element.37), channel_id=1, source_target_pairs={{0,4},{1,5},{2,6},{3,7},{4,0},{5,1},{6,2},{7,3},{8,12},{9,13},{10,... | collective-permute-start | bytes 147464 | tf_op jit(solution)/shard_map/ppermute | solution.py:458
  38.0 1.5 %collective-permute-start.10 = (f32[2,3,2,16,128]{4,3,2,1,0:T(8,128)S(1)}, f32[2,3,2,16,128]{4,3,2,1,0:T(8,128)S(1)}, u32[]{:S(2)}, u32[]{:S(2)}) collective-permute-start(f32[2,3,2,16,128]{4,3,2,1,0:T(8,128)S(1)} %get-tuple-element.30), channel_id=1, source_target_pairs={{0,6},{1,7},{2,0},{3,1},{4,2},{5,3},{6,4},{7,5},{8,14},{9,15},{10,... | collective-permute-start | bytes 294920 | tf_op jit(solution)/shard_map/ppermute | solution.py:458
  39.4 1.0 collective-permute-start.11
  40.4 3.8 %collective-permute-done.7 = f32[1,3,2,16,128]{4,3,2,1,0:T(8,128)S(1)} collective-permute-done((f32[1,3,2,16,128]{4,3,2,1,0:T(8,128)S(1)}, f32[1,3,2,16,128]{4,3,2,1,0:T(8,128)S(1)}, u32[]{:S(2)}, u32[]{:S(2)}) %collective-permute-start.7) | collective-permute-done | bytes 49184 | tf_op jit(solution)/shard_map/ppermute | solution.py:458
  44.2 0.0 collective-permute-start.3
  44.2 0.0 collective-permute-done.6
  44.2 0.6 collective-permute-start.4
  44.8 0.0 collective-permute-done.9
  44.8 7.3 %collective-permute-start.5 = (f32[2,3,2,16,128]{4,3,2,1,0:T(8,128)S(1)}, f32[2,3,2,16,128]{4,3,2,1,0:T(8,128)S(1)}, u32[]{:S(2)}, u32[]{:S(2)}) collective-permute-start(f32[2,3,2,16,128]{4,3,2,1,0:T(8,128)S(1)} %get-tuple-element.32), channel_id=1, source_target_pairs={{0,3},{1,4},{2,5},{3,6},{4,7},{5,0},{6,1},{7,2},{8,11},{9,12},{10,... | collective-permute-start | bytes 294920 | tf_op jit(solution)/shard_map/ppermute | solution.py:458
  52.1 0.0 collective-permute-done.10
  52.1 0.6 collective-permute-start.8
  52.7 0.0 copy-done
  52.7 2.2 %gram.2 = (bf16[96,48,128]{2,1,0:T(8,128)(2,1)S(1)}, f32[16,32]{1,0:T(8,128)S(1)}) custom-call(s32[2]{0:T(128)S(1)} %pad_add_fusion.place, f32[16,96,128]{2,1,0:T(8,128)S(1)} %bitcast.38), custom_call_target="tpu_custom_call" | custom-call | tf_op jit(solution)/shard_map/gram/pallas_call | solution.py:403
  54.8 0.0 collective-permute-done.11
  54.8 0.0 collective-permute-done.3
  54.9 0.0 collective-permute-done.4
  54.9 4.2 %collective-permute-done.5 = f32[2,3,2,16,128]{4,3,2,1,0:T(8,128)S(1)} collective-permute-done((f32[2,3,2,16,128]{4,3,2,1,0:T(8,128)S(1)}, f32[2,3,2,16,128]{4,3,2,1,0:T(8,128)S(1)}, u32[]{:S(2)}, u32[]{:S(2)}) %collective-permute-start.5) | collective-permute-done | bytes 98336 | tf_op jit(solution)/shard_map/ppermute | solution.py:458
  59.1 0.0 collective-permute-done.8
  59.1 2.6 %gram.3 = (bf16[96,48,128]{2,1,0:T(8,128)(2,1)S(1)}, f32[16,32]{1,0:T(8,128)S(1)}) custom-call(s32[2]{0:T(128)S(1)} %pad_add_fusion.place, f32[2,96,128]{2,1,0:T(8,128)S(1)} %bitcast.39, f32[2,96,128]{2,1,0:T(8,128)S(1)} %bitcast.44, f32[2,96,128]{2,1,0:T(8,128)S(1)} %bitcast.45, f32[2,96,128]{2,1,0:T(8,128)S(1)} %bitcast.46, f32[1,96,128]{2,1,0:T(8,128)S(1)} %bitcast.47, ...), custom_call_target="tpu_custom_call" | custom-call | tf_op jit(solution)/shard_map/gram/pallas_call | solution.py:403
  61.7 0.1 pack.1
  61.8 10.8 %all_to_all.10 = f32[16,8,128]{2,1,0:T(8,128)S(1)} all-to-all(f32[16,8,128]{2,1,0:T(8,128)S(1)} %pack.1), channel_id=1, replica_groups=mesh['x'=4,'y'=4,'core'=2,'probe'=8] {'probe','core'}, dimensions={0} | all-to-all | bytes 131072 | tf_op jit(solution)/shard_map/all_to_all | solution.py:494
  72.5 15.2 %all_to_all.11.copies = f32[16,8,128]{2,1,0:T(8,128)S(1)} all-to-all(f32[16,8,128]{2,1,0:T(8,128)S(1)} %broadcast_in_dim.2), channel_id=1, replica_groups=mesh['x'=4,'y'=4,'core'=2,'probe'=8] {'x','y'}, dimensions={0} | all-to-all | bytes 131072 | tf_op jit(solution)/shard_map/all_to_all | solution.py:496
  87.8 4.5 %finish.1 = (f32[1536,128]{1,0:T(8,128)S(1)}, f32[16,16]{1,0:T(8,128)S(1)}) custom-call(s32[2]{0:T(128)S(1)} %pad_add_fusion.place, f32[16,8,128]{2,1,0:T(8,128)S(1)} %all_to_all.11.copies, bf16[96,48,128]{2,1,0:T(8,128)(2,1)S(1)} %get-tuple-element.13.refs_9_.first, bf16[96,48,128]{2,1,0:T(8,128)(2,1)S(1)} %get-tuple-element.15.second, f32[1]{0:T(128)} %constant.18.scale), custom_call_target="tpu_custom_call" | custom-call | tf_op jit(solution)/shard_map/finish/pallas_call | solution.py:431
  92.3 0.7 collective-permute-start.12
  93.1 1.4 %collective-permute-start.16 = (f32[1,3,2,16,128]{4,3,2,1,0:T(8,128)S(1)}, f32[1,3,2,16,128]{4,3,2,1,0:T(8,128)S(1)}, u32[]{:S(2)}, u32[]{:S(2)}) collective-permute-start(f32[1,3,2,16,128]{4,3,2,1,0:T(8,128)S(1)} %bitcast.57), channel_id=1, source_target_pairs={{0,6},{1,7},{2,0},{3,1},{4,2},{5,3},{6,4},{7,5},{8,14},{9,15},{10,... | collective-permute-start | bytes 147464 | tf_op jit(solution)/shard_map/ppermute | solution.py:458
  94.5 3.0 %collective-permute-start.15 = (f32[1,3,2,16,128]{4,3,2,1,0:T(8,128)S(1)}, f32[1,3,2,16,128]{4,3,2,1,0:T(8,128)S(1)}, u32[]{:S(2)}, u32[]{:S(2)}) collective-permute-start(f32[1,3,2,16,128]{4,3,2,1,0:T(8,128)S(1)} %bitcast.56), channel_id=1, source_target_pairs={{0,4},{1,5},{2,6},{3,7},{4,0},{5,1},{6,2},{7,3},{8,12},{9,13},{10,... | collective-permute-start | bytes 147464 | tf_op jit(solution)/shard_map/ppermute | solution.py:458
  97.5 0.6 collective-permute-start.13
  98.0 5.1 %collective-permute-start.14 = (f32[2,3,2,16,128]{4,3,2,1,0:T(8,128)S(1)}, f32[2,3,2,16,128]{4,3,2,1,0:T(8,128)S(1)}, u32[]{:S(2)}, u32[]{:S(2)}) collective-permute-start(f32[2,3,2,16,128]{4,3,2,1,0:T(8,128)S(1)} %bitcast.53), channel_id=1, source_target_pairs={{0,3},{1,4},{2,5},{3,6},{4,7},{5,0},{6,1},{7,2},{8,11},{9,12},{10,... | collective-permute-start | bytes 294920 | tf_op jit(solution)/shard_map/ppermute | solution.py:458
  103.1 0.0 collective-permute-done.16
  103.1 0.0 collective-permute-start.18
  103.1 0.0 collective-permute-done.15.refs_4_
  103.1 3.5 %collective-permute-start.19 = (f32[2,3,2,16,128]{4,3,2,1,0:T(8,128)S(1)}, f32[2,3,2,16,128]{4,3,2,1,0:T(8,128)S(1)}, u32[]{:S(2)}, u32[]{:S(2)}) collective-permute-start(f32[2,3,2,16,128]{4,3,2,1,0:T(8,128)S(1)} %bitcast.51), channel_id=1, source_target_pairs={{0,6},{1,7},{2,0},{3,1},{4,2},{5,3},{6,4},{7,5},{8,14},{9,15},{10,... | collective-permute-start | bytes 294920 | tf_op jit(solution)/shard_map/ppermute | solution.py:458
  106.6 0.0 collective-permute-done.12.refs_1_
  106.6 0.6 collective-permute-start.20
  107.3 3.1 %collective-permute-done.13.refs_2_ = f32[2,3,2,16,128]{4,3,2,1,0:T(8,128)S(1)} collective-permute-done((f32[2,3,2,16,128]{4,3,2,1,0:T(8,128)S(1)}, f32[2,3,2,16,128]{4,3,2,1,0:T(8,128)S(1)}, u32[]{:S(2)}, u32[]{:S(2)}) %collective-permute-start.13) | collective-permute-done | bytes 98336 | tf_op jit(solution)/shard_map/ppermute | solution.py:458
  110.4 0.0 collective-permute-start.17
  110.4 0.7 copy.7
  111.1 0.0 collective-permute-done.14.refs_3_
  111.1 2.6 %collective-permute-done.18.refs_6_ = f32[2,3,2,16,128]{4,3,2,1,0:T(8,128)S(1)} collective-permute-done((f32[2,3,2,16,128]{4,3,2,1,0:T(8,128)S(1)}, f32[2,3,2,16,128]{4,3,2,1,0:T(8,128)S(1)}, u32[]{:S(2)}, u32[]{:S(2)}) %collective-permute-start.18) | collective-permute-done | bytes 98336 | tf_op jit(solution)/shard_map/ppermute | solution.py:458
  113.7 2.2 %collective-permute-done.19.refs_7_ = f32[2,3,2,16,128]{4,3,2,1,0:T(8,128)S(1)} collective-permute-done((f32[2,3,2,16,128]{4,3,2,1,0:T(8,128)S(1)}, f32[2,3,2,16,128]{4,3,2,1,0:T(8,128)S(1)}, u32[]{:S(2)}, u32[]{:S(2)}) %collective-permute-start.19) | collective-permute-done | bytes 98336 | tf_op jit(solution)/shard_map/ppermute | solution.py:458
  115.9 0.9 collective-permute-done.20.refs_8_
  116.8 1.8 %collective-permute-done.17.refs_5_ = f32[1,3,2,16,128]{4,3,2,1,0:T(8,128)S(1)} collective-permute-done((f32[1,3,2,16,128]{4,3,2,1,0:T(8,128)S(1)}, f32[1,3,2,16,128]{4,3,2,1,0:T(8,128)S(1)}, u32[]{:S(2)}, u32[]{:S(2)}) %collective-permute-start.17) | collective-permute-done | bytes 49184 | tf_op jit(solution)/shard_map/ppermute | solution.py:458
  118.6 1.5 %spread.1 = f32[2,3,2,128,128]{4,3,2,1,0:T(8,128)} custom-call(s32[2]{0:T(128)S(1)} %pad_add_fusion.place, f32[2,3,2,16,128]{4,3,2,1,0:T(8,128)S(1)} %bitcast.40, f32[2,3,2,16,128]{4,3,2,1,0:T(8,128)S(1)} %collective-permute-done.12.refs_1_, f32[2,3,2,16,128]{4,3,2,1,0:T(8,128)S(1)} %collective-permute-done.13.refs_2_, ...), custom_call_target="tpu_custom_call" | custom-call | tf_op jit(solution)/shard_map/spread/pallas_call | solution.py:446
  (6 shorter events, 0.1 us)
Async XLA Ops:
  4.0 17.9 %collective-permute-start.2 = (f32[13,128,128]{2,1,0:T(8,128)S(1)}, f32[13,128,128]{2,1,0:T(8,128)S(1)}, u32[]{:S(2)}, u32[]{:S(2)}) collective-permute-start(f32[13,128,128]{2,1,0:T(8,128)S(1)} %get-tuple-element.12.up), channel_id=1, source_target_pairs={{0,8},{8,0},{1,9},{9,1},{2,10},{10,2},{3,11},{11,3},{4,12},{12,4},... | collective-permute-start | bytes 2555912 | tf_op jit(solution)/shard_map/ppermute | solution.py:485
  5.8 16.2 %collective-permute-start = (f32[7,128,128]{2,1,0:T(8,128)S(1)}, f32[7,128,128]{2,1,0:T(8,128)S(1)}, u32[]{:S(2)}, u32[]{:S(2)}) collective-permute-start(f32[7,128,128]{2,1,0:T(8,128)S(1)} %lift.1.down), channel_id=1, source_target_pairs={{8,16},{24,32},{40,48},{56,64},{72,80},{88,96},{104,112},{120,128}... | collective-permute-start | bytes 1376264 | tf_op jit(solution)/shard_map/ppermute | solution.py:482
  10.8 11.2 %collective-permute-start.1 = (f32[6,128,128]{2,1,0:T(8,128)S(1)}, f32[6,128,128]{2,1,0:T(8,128)S(1)}, u32[]{:S(2)}, u32[]{:S(2)}) collective-permute-start(f32[6,128,128]{2,1,0:T(8,128)S(1)} %get-tuple-element.11.down_part), channel_id=1, source_target_pairs={{8,16},{24,32},{40,48},{56,64},{72,80},{88,96},{104,112},{120,128}... | collective-permute-start | bytes 1179656 | tf_op jit(solution)/shard_map/ppermute | solution.py:484
  25.9 26.7 %copy-start = (f32[16,3,2,16,128]{4,3,2,1,0:T(8,128)S(1)}, f32[16,3,2,16,128]{4,3,2,1,0:T(8,128)}, u32[]{:S(2)}) copy-start(f32[16,3,2,16,128]{4,3,2,1,0:T(8,128)} %param.6) | copy-start | bytes 2359300
  26.0 18.8 %collective-permute-start.9 = (f32[2,3,2,16,128]{4,3,2,1,0:T(8,128)S(1)}, f32[2,3,2,16,128]{4,3,2,1,0:T(8,128)S(1)}, u32[]{:S(2)}, u32[]{:S(2)}) collective-permute-start(f32[2,3,2,16,128]{4,3,2,1,0:T(8,128)S(1)} %get-tuple-element.31), channel_id=1, source_target_pairs={{0,5},{1,6},{2,7},{3,0},{4,1},{5,2},{6,3},{7,4},{8,13},{9,14},{10,... | collective-permute-start | bytes 294920 | tf_op jit(solution)/shard_map/ppermute | solution.py:458
  32.8 11.3 %collective-permute-start.7 = (f32[1,3,2,16,128]{4,3,2,1,0:T(8,128)S(1)}, f32[1,3,2,16,128]{4,3,2,1,0:T(8,128)S(1)}, u32[]{:S(2)}, u32[]{:S(2)}) collective-permute-start(f32[1,3,2,16,128]{4,3,2,1,0:T(8,128)S(1)} %get-tuple-element.36), channel_id=1, source_target_pairs={{0,6},{1,7},{2,0},{3,1},{4,2},{5,3},{6,4},{7,5},{8,14},{9,15},{10,... | collective-permute-start | bytes 147464 | tf_op jit(solution)/shard_map/ppermute | solution.py:458
  33.5 10.7 %collective-permute-start.6 = (f32[1,3,2,16,128]{4,3,2,1,0:T(8,128)S(1)}, f32[1,3,2,16,128]{4,3,2,1,0:T(8,128)S(1)}, u32[]{:S(2)}, u32[]{:S(2)}) collective-permute-start(f32[1,3,2,16,128]{4,3,2,1,0:T(8,128)S(1)} %get-tuple-element.37), channel_id=1, source_target_pairs={{0,4},{1,5},{2,6},{3,7},{4,0},{5,1},{6,2},{7,3},{8,12},{9,13},{10,... | collective-permute-start | bytes 147464 | tf_op jit(solution)/shard_map/ppermute | solution.py:458
  38.0 14.1 %collective-permute-start.10 = (f32[2,3,2,16,128]{4,3,2,1,0:T(8,128)S(1)}, f32[2,3,2,16,128]{4,3,2,1,0:T(8,128)S(1)}, u32[]{:S(2)}, u32[]{:S(2)}) collective-permute-start(f32[2,3,2,16,128]{4,3,2,1,0:T(8,128)S(1)} %get-tuple-element.30), channel_id=1, source_target_pairs={{0,6},{1,7},{2,0},{3,1},{4,2},{5,3},{6,4},{7,5},{8,14},{9,15},{10,... | collective-permute-start | bytes 294920 | tf_op jit(solution)/shard_map/ppermute | solution.py:458
  39.4 15.4 %collective-permute-start.11 = (f32[2,3,2,16,128]{4,3,2,1,0:T(8,128)S(1)}, f32[2,3,2,16,128]{4,3,2,1,0:T(8,128)S(1)}, u32[]{:S(2)}, u32[]{:S(2)}) collective-permute-start(f32[2,3,2,16,128]{4,3,2,1,0:T(8,128)S(1)} %get-tuple-element.29), channel_id=1, source_target_pairs={{0,7},{1,0},{2,1},{3,2},{4,3},{5,4},{6,5},{7,6},{8,15},{9,8},{10,9... | collective-permute-start | bytes 294920 | tf_op jit(solution)/shard_map/ppermute | solution.py:458
  44.2 10.7 %collective-permute-start.3 = (f32[2,3,2,16,128]{4,3,2,1,0:T(8,128)S(1)}, f32[2,3,2,16,128]{4,3,2,1,0:T(8,128)S(1)}, u32[]{:S(2)}, u32[]{:S(2)}) collective-permute-start(f32[2,3,2,16,128]{4,3,2,1,0:T(8,128)S(1)} %get-tuple-element.34), channel_id=1, source_target_pairs={{0,1},{1,2},{2,3},{3,4},{4,5},{5,6},{6,7},{7,0},{8,9},{9,10},{10,1... | collective-permute-start | bytes 294920 | tf_op jit(solution)/shard_map/ppermute | solution.py:458
  44.2 10.7 %collective-permute-start.4 = (f32[2,3,2,16,128]{4,3,2,1,0:T(8,128)S(1)}, f32[2,3,2,16,128]{4,3,2,1,0:T(8,128)S(1)}, u32[]{:S(2)}, u32[]{:S(2)}) collective-permute-start(f32[2,3,2,16,128]{4,3,2,1,0:T(8,128)S(1)} %get-tuple-element.33), channel_id=1, source_target_pairs={{0,2},{1,3},{2,4},{3,5},{4,6},{5,7},{6,0},{7,1},{8,10},{9,11},{10,... | collective-permute-start | bytes 294920 | tf_op jit(solution)/shard_map/ppermute | solution.py:458
  44.8 14.3 %collective-permute-start.5 = (f32[2,3,2,16,128]{4,3,2,1,0:T(8,128)S(1)}, f32[2,3,2,16,128]{4,3,2,1,0:T(8,128)S(1)}, u32[]{:S(2)}, u32[]{:S(2)}) collective-permute-start(f32[2,3,2,16,128]{4,3,2,1,0:T(8,128)S(1)} %get-tuple-element.32), channel_id=1, source_target_pairs={{0,3},{1,4},{2,5},{3,6},{4,7},{5,0},{6,1},{7,2},{8,11},{9,12},{10,... | collective-permute-start | bytes 294920 | tf_op jit(solution)/shard_map/ppermute | solution.py:458
  52.1 7.0 %collective-permute-start.8 = (f32[1,3,2,16,128]{4,3,2,1,0:T(8,128)S(1)}, f32[1,3,2,16,128]{4,3,2,1,0:T(8,128)S(1)}, u32[]{:S(2)}, u32[]{:S(2)}) collective-permute-start(f32[1,3,2,16,128]{4,3,2,1,0:T(8,128)S(1)} %collective-permute-done.7), channel_id=1, source_target_pairs={{0,6},{1,7},{2,0},{3,1},{4,2},{5,3},{6,4},{7,5},{8,14},{9,15},{10,... | collective-permute-start | bytes 147464 | tf_op jit(solution)/shard_map/ppermute | solution.py:458
  92.3 14.3 %collective-permute-start.12 = (f32[2,3,2,16,128]{4,3,2,1,0:T(8,128)S(1)}, f32[2,3,2,16,128]{4,3,2,1,0:T(8,128)S(1)}, u32[]{:S(2)}, u32[]{:S(2)}) collective-permute-start(f32[2,3,2,16,128]{4,3,2,1,0:T(8,128)S(1)} %bitcast.55), channel_id=1, source_target_pairs={{0,1},{1,2},{2,3},{3,4},{4,5},{5,6},{6,7},{7,0},{8,9},{9,10},{10,1... | collective-permute-start | bytes 294920 | tf_op jit(solution)/shard_map/ppermute | solution.py:458
  93.1 10.1 %collective-permute-start.16 = (f32[1,3,2,16,128]{4,3,2,1,0:T(8,128)S(1)}, f32[1,3,2,16,128]{4,3,2,1,0:T(8,128)S(1)}, u32[]{:S(2)}, u32[]{:S(2)}) collective-permute-start(f32[1,3,2,16,128]{4,3,2,1,0:T(8,128)S(1)} %bitcast.57), channel_id=1, source_target_pairs={{0,6},{1,7},{2,0},{3,1},{4,2},{5,3},{6,4},{7,5},{8,14},{9,15},{10,... | collective-permute-start | bytes 147464 | tf_op jit(solution)/shard_map/ppermute | solution.py:458
  94.5 8.7 %collective-permute-start.15 = (f32[1,3,2,16,128]{4,3,2,1,0:T(8,128)S(1)}, f32[1,3,2,16,128]{4,3,2,1,0:T(8,128)S(1)}, u32[]{:S(2)}, u32[]{:S(2)}) collective-permute-start(f32[1,3,2,16,128]{4,3,2,1,0:T(8,128)S(1)} %bitcast.56), channel_id=1, source_target_pairs={{0,4},{1,5},{2,6},{3,7},{4,0},{5,1},{6,2},{7,3},{8,12},{9,13},{10,... | collective-permute-start | bytes 147464 | tf_op jit(solution)/shard_map/ppermute | solution.py:458
  97.5 12.9 %collective-permute-start.13 = (f32[2,3,2,16,128]{4,3,2,1,0:T(8,128)S(1)}, f32[2,3,2,16,128]{4,3,2,1,0:T(8,128)S(1)}, u32[]{:S(2)}, u32[]{:S(2)}) collective-permute-start(f32[2,3,2,16,128]{4,3,2,1,0:T(8,128)S(1)} %bitcast.54), channel_id=1, source_target_pairs={{0,2},{1,3},{2,4},{3,5},{4,6},{5,7},{6,0},{7,1},{8,10},{9,11},{10,... | collective-permute-start | bytes 294920 | tf_op jit(solution)/shard_map/ppermute | solution.py:458
  98.0 13.0 %collective-permute-start.14 = (f32[2,3,2,16,128]{4,3,2,1,0:T(8,128)S(1)}, f32[2,3,2,16,128]{4,3,2,1,0:T(8,128)S(1)}, u32[]{:S(2)}, u32[]{:S(2)}) collective-permute-start(f32[2,3,2,16,128]{4,3,2,1,0:T(8,128)S(1)} %bitcast.53), channel_id=1, source_target_pairs={{0,3},{1,4},{2,5},{3,6},{4,7},{5,0},{6,1},{7,2},{8,11},{9,12},{10,... | collective-permute-start | bytes 294920 | tf_op jit(solution)/shard_map/ppermute | solution.py:458
  103.1 10.5 %collective-permute-start.18 = (f32[2,3,2,16,128]{4,3,2,1,0:T(8,128)S(1)}, f32[2,3,2,16,128]{4,3,2,1,0:T(8,128)S(1)}, u32[]{:S(2)}, u32[]{:S(2)}) collective-permute-start(f32[2,3,2,16,128]{4,3,2,1,0:T(8,128)S(1)} %bitcast.52), channel_id=1, source_target_pairs={{0,5},{1,6},{2,7},{3,0},{4,1},{5,2},{6,3},{7,4},{8,13},{9,14},{10,... | collective-permute-start | bytes 294920 | tf_op jit(solution)/shard_map/ppermute | solution.py:458
  103.1 12.8 %collective-permute-start.19 = (f32[2,3,2,16,128]{4,3,2,1,0:T(8,128)S(1)}, f32[2,3,2,16,128]{4,3,2,1,0:T(8,128)S(1)}, u32[]{:S(2)}, u32[]{:S(2)}) collective-permute-start(f32[2,3,2,16,128]{4,3,2,1,0:T(8,128)S(1)} %bitcast.51), channel_id=1, source_target_pairs={{0,6},{1,7},{2,0},{3,1},{4,2},{5,3},{6,4},{7,5},{8,14},{9,15},{10,... | collective-permute-start | bytes 294920 | tf_op jit(solution)/shard_map/ppermute | solution.py:458
  106.6 10.2 %collective-permute-start.20 = (f32[2,3,2,16,128]{4,3,2,1,0:T(8,128)S(1)}, f32[2,3,2,16,128]{4,3,2,1,0:T(8,128)S(1)}, u32[]{:S(2)}, u32[]{:S(2)}) collective-permute-start(f32[2,3,2,16,128]{4,3,2,1,0:T(8,128)S(1)} %bitcast.50), channel_id=1, source_target_pairs={{0,7},{1,0},{2,1},{3,2},{4,3},{5,4},{6,5},{7,6},{8,15},{9,8},{10,9... | collective-permute-start | bytes 294920 | tf_op jit(solution)/shard_map/ppermute | solution.py:458
  110.4 8.3 %collective-permute-start.17 = (f32[1,3,2,16,128]{4,3,2,1,0:T(8,128)S(1)}, f32[1,3,2,16,128]{4,3,2,1,0:T(8,128)S(1)}, u32[]{:S(2)}, u32[]{:S(2)}) collective-permute-start(f32[1,3,2,16,128]{4,3,2,1,0:T(8,128)S(1)} %collective-permute-done.16), channel_id=1, source_target_pairs={{0,6},{1,7},{2,0},{3,1},{4,2},{5,3},{6,4},{7,5},{8,14},{9,15},{10,... | collective-permute-start | bytes 147464 | tf_op jit(solution)/shard_map/ppermute | solution.py:458
where the time goes:
time: 121 us; the launch traced here: 120 us
  starting transfers between devices  45.6 us (38%)
  waiting for transfers between devices  27.2 us (22%)
  blocking collectives  26 us (21%)
  Pallas kernels  19.7 us (16%)
    ppermute x18, starting transfers between devices, shift(): lax.ppermute(block, 'probe', [(j, (j + by) % columns) for j in range(colu...  37.8 us
    ppermute x18, waiting for transfers between devices, shift(): lax.ppermute(block, 'probe', [(j, (j + by) % columns) for j in range(colu...  18.7 us
    all_to_all x1, blocking collectives, body(): copies = lax.all_to_all(copies, ('x', 'y'), 0, 0, tiled=True)  15.2 us
    all_to_all x1, blocking collectives, body(): copies = lax.all_to_all(copies, ('probe', 'core'), 0, 0, tiled=True)  10.8 us
    ppermute x1, waiting for transfers between devices, body(): got_far = lax.ppermute(far, places, outer)  8.52 us
    ppermute x1, starting transfers between devices, body(): got_raw = lax.ppermute(raw, places, outer)  4.99 us
    pallas_call x2, Pallas kernels, gram_call(): pl.pallas_call(functools.partial(gram_kernel, pieces=pieces, alone=alone)...  4.76 us
    pallas_call x1, Pallas kernels, finish_call(): pl.pallas_call(finish_kernel, out_shape=(pltpu.VMEM((16 * length, breadth...  4.47 us
  transfers between devices with their start and end apart: 21, of which 8 were waited for; matrix products, arithmetic and copies ran while one was open for 1% of the time, Pallas kernels for 3%

commit v1 on v0

--- a/solution.py
+++ b/solution.py
@@ -57,9 +57,9 @@
     )
 
 
-def lift_kernel(place, probes_far, modulus_far, out, sems):
+def lift_kernel(probes_far, modulus_far, out, sems):
     count = probes_far.shape[0]
-    core = place[0]
+    core = lax.axis_index("core")
     copies = [
         pltpu.make_async_copy(probes_far.at[k, :, core], out.at[pl.ds(3 * k, 3)], sems.at[k]) for k in range(count)
     ]
@@ -70,53 +70,38 @@
         copy.wait()
 
 
-def partial_kernel(place, probes_far, modulus_far, tangent_far, far, near, probes, modulus, tangent, prod, sems):
+def partial_kernel(probes, modulus, tangent, far, near, prod):
     count = probes.shape[0]
     height = probes.shape[3]
-    core = place[0]
-    copies = []
-    for z, plane in ((0, core), (1, 1 - core)):
-        triples = (
-            (modulus_far.at[pl.ds(plane, 1)], modulus.at[pl.ds(z, 1)]),
-            (probes_far.at[:, :, pl.ds(plane, 1)], probes.at[:, :, pl.ds(z, 1)]),
-            (tangent_far.at[:, pl.ds(plane, 1)], tangent.at[:, pl.ds(z, 1)]),
-        )
-        copies.append([pltpu.make_async_copy(src, dst, sems.at[z, n]) for n, (src, dst) in enumerate(triples)])
-    for n in range(3):
-        copies[0][n].start()
-        copies[1][n].start()
-    for n in range(2):
-        copies[0][n].wait()
-        copies[1][n].wait()
+    core = lax.axis_index("core")
+    depth = (core, 1 - core)
     for z in range(2):
         for k in range(count):
             for i in range(3):
-                prod[z * 3 * count + 3 * k + i] = probes[k, i, z] * modulus[z]
-    copies[0][2].wait()
-    copies[1][2].wait()
+                prod[z * 3 * count + 3 * k + i] = probes[k, i, depth[z]] * modulus[depth[z]]
     for z, out in ((0, far), (1, near)):
         other = 1 - z
         for s in range(0, height, STRIP):
             here = pl.ds(s, STRIP)
 
             def mod(plane, shift):
-                return rows_at(modulus, (plane,), s, shift, height)
+                return rows_at(modulus, (depth[plane],), s, shift, height)
 
             m = mod(z, 0)
             side = mod(other, 0)
             neighbours = full_sum(m, mod(z, -1) + mod(z, 1), side, mod(other, -1) + mod(other, 1))
             common = (3.4 / 16.0) * m + PART * neighbours - 1.0
-            diag = [common + 0.125 * tangent[i, z, here, :] for i in range(3)]
-            off = [0.125 * tangent[3 + i, z, here, :] for i in range(3)]
+            diag = [common + 0.125 * tangent[i, depth[z], here, :] for i in range(3)]
+            off = [0.125 * tangent[3 + i, depth[z], here, :] for i in range(3)]
             scaled = PART * m
             if z:
                 out[6 * count, here, :] = m
             for k in range(count):
-                values = [probes[k, i, z, here, :] for i in range(3)]
+                values = [probes[k, i, depth[z], here, :] for i in range(3)]
                 mixed = combine(diag, off, values)
                 for i in range(3):
                     def val(plane, shift):
-                        return rows_at(probes, (k, i, plane), s, shift, height)
+                        return rows_at(probes, (k, i, depth[plane]), s, shift, height)
 
                     def pro(plane, shift):
                         return rows_at(prod, (plane * 3 * count + 3 * k + i,), s, shift, height)
@@ -128,26 +113,19 @@
                     out[3 * count * z + 3 * k + i, here, :] = mixed[i] - scaled * first - PART * second
 
 
-def filter_kernel(place, lo, lo_part, down, down_part, up, hi, tangent_far, out, tangent, once, prod, sums, products, prior, sems):
+def filter_kernel(lo, lo_part, down, down_part, up, hi, tangent, out, once, prod, sums, products, prior):
     planes = (lo, down, up, hi)
-    core = place[0]
+    core = lax.axis_index("core")
     parts = (lo_part, down_part, up, hi)
-    copies = [
-        pltpu.make_async_copy(tangent_far.at[:, pl.ds(plane, 1)], tangent.at[:, pl.ds(z, 1)], sems.at[z])
-        for z, plane in ((0, core), (1, 1 - core))
-    ]
-    for copy in copies:
-        copy.start()
     total = lo.shape[0] - 1
     count = total // 3
     height = lo.shape[1]
     blocks = height // STRIP
     last = (total, total, 2 * total, 2 * total)
     start = (0, 0, total, total)
-    mods = [planes[z][last[z]] for z in range(4)]
     for z in range(4):
         for n in range(total):
-            prior[z * total + n] = planes[z][n] * mods[z]
+            prior[z * total + n] = planes[z][n] * planes[z][last[z]]
     for source, target in ((0, 1), (1, 0), (2, 3), (3, 2)):
         src = planes[source]
         dst = planes[target]
@@ -173,8 +151,6 @@
         for n in range(total):
             sums[(z - 1) * total + n] = once[(z - 1) * total + n] + once[(z + 1) * total + n]
             products[(z - 1) * total + n] = prod[(z - 1) * total + n] + prod[(z + 1) * total + n]
-    for copy in copies:
-        copy.wait()
     for z, depth in ((1, core), (2, 1 - core)):
         plane = planes[z]
         for s in range(0, height, STRIP):
@@ -190,10 +166,10 @@
             side = [mod(z - 1, d) + mod(z + 1, d) for d in (-1, 0, 1)]
             neighbours = full_sum(m, mod(z, -1) + mod(z, 1), side[1], side[0] + side[2])
             common = (6.8 / 16.0) * m + (2.0 * PART) * neighbours - 2.0
-            diag = [common + 0.25 * tangent[i, z - 1, here, :] for i in range(3)]
-            off = [0.25 * tangent[3 + i, z - 1, here, :] for i in range(3)]
+            diag = [common + 0.25 * tangent[i, depth, here, :] for i in range(3)]
+            off = [0.25 * tangent[3 + i, depth, here, :] for i in range(3)]
             scaled = (2.0 * PART) * m
-            turn = lax.rem(s // STRIP + blocks - place[1], blocks)
+            turn = lax.rem(s // STRIP + blocks - lax.axis_index("probe"), blocks)
             for k in range(count):
                 base = z * total + 3 * k
                 mixed = combine(diag, off, [once[base + i, here, :] for i in range(3)])
@@ -228,7 +204,7 @@
 WIDE = 8
 
 
-def gram_kernel(place, *refs, pieces, alone):
+def gram_kernel(*refs, pieces, alone):
     stack, out, tall = refs[-3:]
     chunks = refs[: len(pieces)]
     earlier = refs[len(pieces) : -3]
@@ -238,7 +214,7 @@
         each = chunk.shape[0]
         base = first
         if not alone:
-            source = place[1] - turn
+            source = lax.axis_index("probe") - turn
             base = first + 2 * jnp.where(source < 0, source + count // 2, source)
         for j in range(each):
             tall[pl.ds(base + j, length, stride=count), :] = chunk[j]
@@ -271,7 +247,7 @@
         out[n] = packed
 
 
-def finish_kernel(place, copies, first, second, scale, out, correlation):
+def finish_kernel(copies, first, second, out, correlation, *, factor):
     length = first.shape[0]
     kept = first.shape[1] // 3
     made = second.shape[1] // 3
@@ -289,7 +265,6 @@
     work = jnp.concatenate([gram, unit, jnp.zeros((total, 128 - 2 * total), jnp.float32)], axis=1)
     slot = lax.broadcasted_iota(jnp.int32, (total, 1), 0)
     pivots = jnp.zeros((total, 1), jnp.float32)
-    factor = scale[0]
     for k in range(total):
         if k == kept:
             correlation[...] = -factor * work[kept:, total : total + kept]
@@ -300,7 +275,7 @@
     weights = factor * work[kept:, total : 2 * total] * lax.rsqrt(pivots[kept:])
     there = lax.broadcasted_iota(jnp.int32, (made, made), 0)
     source = lax.broadcasted_iota(jnp.int32, (made, made), 1)
-    moved = there + 2 * place[1]
+    moved = there + 2 * lax.axis_index("probe")
     turn = jnp.where(jnp.where(moved >= made, moved - made, moved) == source, 1.0, 0.0)
     weights = jnp.dot(turn, weights, precision=lax.Precision.HIGHEST)
     lines = []
@@ -325,12 +300,12 @@
     return listed
 
 
-def spread_kernel(place, *refs):
+def spread_kernel(*refs):
     blocks, out, sems = refs[:-2], refs[-2], refs[-1]
     turns = len(blocks) - 1
     copies = []
     for n, (block, k, first) in enumerate(out_turns(blocks)):
-        source = lax.rem(place[1] + turns - k, turns)
+        source = lax.rem(lax.axis_index("probe") + turns - k, turns)
         target = out.at[pl.ds(first, block.shape[0]), :, :, pl.ds(source * STRIP, STRIP), :]
         copies.append(pltpu.make_async_copy(block, target, sems.at[n]))
     for copy in copies:
@@ -340,7 +315,6 @@
 
 
 VM = pl.BlockSpec(memory_space=pltpu.VMEM)
-SM = pl.BlockSpec(memory_space=pltpu.SMEM)
 FAR = pl.BlockSpec(memory_space=pltpu.HBM)
 
 
@@ -352,51 +326,49 @@
     return tuple(pltpu.with_memory_space_constraint(a, pltpu.HBM) for a in arrays)
 
 
-def lift_call(place, probes, modulus):
+def lift_call(probes, modulus):
     count, _, _, height, breadth = probes.shape
     return pl.pallas_call(
         lift_kernel,
         out_shape=pltpu.VMEM((3 * count + 1, height, breadth), jnp.float32),
-        in_specs=[SM, FAR, FAR],
+        in_specs=[FAR, FAR],
         out_specs=VM,
         scratch_shapes=[pltpu.SemaphoreType.DMA((count + 1,))],
         compiler_params=pltpu.CompilerParams(vmem_limit_bytes=1 << 20),
         name="lift",
-    )(place, *in_far(probes, modulus))
-
-
-def partial_call(place, probes, modulus, tangent):
+    )(*in_far(probes, modulus))
+
+
+def partial_call(probes, modulus, tangent):
     count, _, _, height, breadth = probes.shape
     plane = lambda n: pltpu.VMEM((n, height, breadth), jnp.float32)
     return pl.pallas_call(
         partial_kernel,
         out_shape=(plane(3 * count), plane(6 * count + 1)),
-        in_specs=[SM] + [FAR] * 3,
+        in_specs=[VM] * 3,
         out_specs=(VM, VM),
-        scratch_shapes=[pltpu.VMEM(a.shape, jnp.float32) for a in (probes, modulus, tangent)]
-        + [plane(6 * count), pltpu.SemaphoreType.DMA((2, 3))],
+        scratch_shapes=[plane(6 * count)],
         compiler_params=pltpu.CompilerParams(vmem_limit_bytes=12 << 20),
         name="partial",
-    )(place, *in_far(probes, modulus, tangent))
-
-
-def filter_call(place, packs, tangent):
+    )(*near_chip(probes, modulus, tangent))
+
+
+def filter_call(packs, tangent):
     packed, height, breadth = packs[0].shape
     total = packed - 1
     plane = lambda n: pltpu.VMEM((n, height, breadth), jnp.float32)
     return pl.pallas_call(
         filter_kernel,
         out_shape=pltpu.VMEM((height // STRIP, total // 3, 3, 2, STRIP, breadth), jnp.float32),
-        in_specs=[SM] + [VM] * len(packs) + [FAR],
+        in_specs=[VM] * (len(packs) + 1),
         out_specs=VM,
-        scratch_shapes=[pltpu.VMEM(tangent.shape, jnp.float32), plane(4 * total), plane(4 * total)]
-        + [plane(2 * total), plane(2 * total), plane(4 * total), pltpu.SemaphoreType.DMA((2,))],
+        scratch_shapes=[plane(n * total) for n in (4, 4, 2, 2, 4)],
         compiler_params=pltpu.CompilerParams(vmem_limit_bytes=16 << 20),
         name="filter",
-    )(place, *near_chip(*packs), *in_far(tangent))
-
-
-def gram_call(place, chunks, pieces, earlier=()):
+    )(*near_chip(*packs, tangent))
+
+
+def gram_call(chunks, pieces, earlier=()):
     alone = not earlier
     length, breadth = chunks[0].shape[1:]
     count = sum(c.shape[0] for c in chunks)
@@ -406,12 +378,12 @@
             pltpu.VMEM((length, 3 * count, breadth), jnp.bfloat16),
             pltpu.VMEM((count, 2 * count), jnp.float32),
         ),
-        in_specs=[SM] + [VM] * (len(chunks) + len(earlier)),
+        in_specs=[VM] * (len(chunks) + len(earlier)),
         out_specs=(VM, VM),
         scratch_shapes=[pltpu.VMEM((length * count, breadth), jnp.float32)],
         compiler_params=pltpu.CompilerParams(vmem_limit_bytes=8 << 20),
         name="gram",
-    )(place, *near_chip(*chunks, *earlier))
+    )(*near_chip(*chunks, *earlier))
 
 
 def pack_call(grams, copies):
@@ -426,32 +398,32 @@
     )(*near_chip(*grams))
 
 
-def finish_call(place, copies, stacks, scale):
+def finish_call(copies, stacks, scale):
     length, _, breadth = stacks[0].shape
     return pl.pallas_call(
-        finish_kernel,
+        functools.partial(finish_kernel, factor=scale),
         out_shape=(
             pltpu.VMEM((16 * length, breadth), jnp.float32),
             jax.ShapeDtypeStruct((16, 16), jnp.float32),
         ),
-        in_specs=[SM] + [VM] * 3 + [SM],
+        in_specs=[VM] * 3,
         out_specs=(VM, VM),
         compiler_params=pltpu.CompilerParams(vmem_limit_bytes=8 << 20),
         name="finish",
-    )(place, *near_chip(copies, *stacks), scale)
-
-
-def spread_call(place, blocks):
+    )(*near_chip(copies, *stacks))
+
+
+def spread_call(blocks):
     count, parts, depth, strip, breadth = blocks[0].shape
     return pl.pallas_call(
         spread_kernel,
         out_shape=jax.ShapeDtypeStruct((count, parts, depth, strip * (len(blocks) - 1), breadth), jnp.float32),
-        in_specs=[SM] + [VM] * len(blocks),
+        in_specs=[VM] * len(blocks),
         out_specs=FAR,
         scratch_shapes=[pltpu.SemaphoreType.DMA((len(blocks),))],
         compiler_params=pltpu.CompilerParams(vmem_limit_bytes=8 << 20),
         name="spread",
-    )(place, *near_chip(*blocks))
+    )(*near_chip(*blocks))
 
 
 def shift(block, by, columns):
@@ -475,29 +447,28 @@
     kept = earlier.shape[0]
     breadth = earlier.shape[-1]
     length = math.prod(earlier.shape[1:-1])
-    place = jnp.stack([lax.axis_index("core"), lax.axis_index("probe")]).astype(jnp.int32)
     places = ("x", "y", "core")
     outer = [(i, i + 1) for i in range(1, slabs - 1, 2)] + [(i, i - 1) for i in range(2, slabs, 2)]
-    raw = lift_call(place, probes, modulus)
+    raw = lift_call(probes, modulus)
     got_raw = lax.ppermute(raw, places, outer)
-    far, near = partial_call(place, probes, modulus, tangent)
+    far, near = partial_call(probes, modulus, tangent)
     got_far = lax.ppermute(far, places, outer)
     got_near = lax.ppermute(near, "core", [(0, 1), (1, 0)])
-    first, first_gram = gram_call(place, [earlier.reshape(kept, length, breadth)], ((0, 0),))
-    filtered = filter_call(place, (got_raw, got_far, raw, far, near, got_near), tangent)
+    first, first_gram = gram_call([earlier.reshape(kept, length, breadth)], ((0, 0),))
+    filtered = filter_call((got_raw, got_far, raw, far, near, got_near), tangent)
     got = exchange([filtered[k] for k in range(columns)], columns)
     half = columns // 2
     pieces = [(k, 0) for k in range(half + 1)] + [(half, 1)] + [(k, 0) for k in range(half + 1, columns)]
     flat = [g.reshape(g.shape[0], length, breadth) for g in got]
-    second, second_gram = gram_call(place, flat, tuple(pieces), (first,))
+    second, second_gram = gram_call(flat, tuple(pieces), (first,))
     copies = pack_call((first_gram, second_gram), 2 * columns)
     copies = lax.all_to_all(copies, ("probe", "core"), 0, 0, tiled=True)
     copies = jnp.broadcast_to(jnp.sum(copies, axis=0, keepdims=True), (slabs // 2,) + copies.shape[1:])
     copies = lax.all_to_all(copies, ("x", "y"), 0, 0, tiled=True)
-    rows, correlation = finish_call(place, copies, (first, second), scale.reshape(1))
+    rows, correlation = finish_call(copies, (first, second), scale)
     rows = rows.reshape((columns, 2) + earlier.shape[1:])
     got = exchange([rows[k] for k in range(columns)], columns)
-    basis = spread_call(place, got)
+    basis = spread_call(got)
     return (basis, correlation.T)
 
 
@@ -517,7 +488,7 @@
 
     def step(probes, earlier, modulus, tangent):
         length = math.prod(probes.shape[1:])
-        scale = jnp.sqrt(jnp.float32(length))
+        scale = math.sqrt(length)
         inner = lambda *parts: body(*parts, slabs, columns, scale)
         return jax.shard_map(inner, mesh=wide, in_specs=in_specs, out_specs=out_specs, check_vma=False)(
             probes, earlier, modulus, tangent

time: 121 us -> 119 us (0.983)
  Pallas kernels: 19.7 us -> 14.4 us
  local copies, waits for them, and re-layouts: 0.79 us -> 3.96 us
    unnamed x3 -> x11, local copies, waits for them, and re-layouts: 0.68 us -> 3.84 us
    pallas_call x1, Pallas kernels: 3.33 us -> 1.45 us  [partial_call(): pl.pallas_call(partial_kernel, out_shape=(plane(3 * count), plane(6 * cou...]
  transfers between devices with their start and end apart: 21 -> 21, of which waited for: 8 -> 8; matrix products, arithmetic and copies ran while one was open for 1% -> 1% of each run, Pallas kernels for 3% -> 2%
where the time goes in v1:
time: 119 us
  starting transfers between devices  45.6 us (38%)
  waiting for transfers between devices  27.7 us (23%)
  blocking collectives  26.1 us (22%)
  Pallas kernels  14.4 us (12%)
  local copies, waits for them, and re-layouts  3.96 us (3%)
    ppermute x18, starting transfers between devices, shift(): lax.ppermute(block, 'probe', [(j, (j + by) % columns) for j in range(colu...  37.8 us
    ppermute x18, waiting for transfers between devices, shift(): lax.ppermute(block, 'probe', [(j, (j + by) % columns) for j in range(colu...  19.2 us
    all_to_all x1, blocking collectives, body(): copies = lax.all_to_all(copies, ('x', 'y'), 0, 0, tiled=True)  15.3 us
    all_to_all x1, blocking collectives, body(): copies = lax.all_to_all(copies, ('probe', 'core'), 0, 0, tiled=True)  10.8 us
    ppermute x1, waiting for transfers between devices, body(): got_far = lax.ppermute(far, places, outer)  8.51 us
    ppermute x1, starting transfers between devices, body(): got_raw = lax.ppermute(raw, places, outer)  4.98 us
    pallas_call x1, Pallas kernels, finish_call(): pl.pallas_call(functools.partial(finish_kernel, factor=scale), out_shape=...  3.93 us
    unnamed x11, local copies, waits for them, and re-layouts  3.84 us
  transfers between devices with their start and end apart: 21, of which 8 were waited for; matrix products, arithmetic and copies ran while one was open for 1% of the time, Pallas kernels for 2%

profile of v1, /device:TPU:2, one launch (start us, length us, event | category | flops | bytes accessed | tf_op | source)
XLA Modules:
  0.0 118.6 jit_solution(13488886256643792747)
XLA Ops:
  0.6 0.0 copy-start
  0.6 1.1 copy-done
  1.8 0.0 copy-start.2
  1.8 1.1 copy-done.2
  2.9 0.0 copy-start.4
  2.9 0.9 copy-done.4
  3.8 0.0 copy-start.1
  3.8 1.5 %partial.1 = (f32[6,128,128]{2,1,0:T(8,128)S(1)}, f32[13,128,128]{2,1,0:T(8,128)S(1)}) custom-call(f32[2,3,2,128,128]{4,3,2,1,0:T(8,128)S(1)} %copy-done.2, f32[2,128,128]{2,1,0:T(8,128)S(1)} %copy-done.4, f32[6,2,128,128]{3,2,1,0:T(8,128)S(1)} %copy-done), custom_call_target="tpu_custom_call" | custom-call | tf_op jit(solution)/shard_map/partial/pallas_call | solution.py:345
  5.3 0.1 collective-permute-start.2
  5.4 1.1 lift.1.down
  6.4 5.0 %collective-permute-start = (f32[7,128,128]{2,1,0:T(8,128)S(1)}, f32[7,128,128]{2,1,0:T(8,128)S(1)}, u32[]{:S(2)}, u32[]{:S(2)}) collective-permute-start(f32[7,128,128]{2,1,0:T(8,128)S(1)} %lift.1.down), channel_id=1, source_target_pairs={{8,16},{24,32},{40,48},{56,64},{72,80},{88,96},{104,112},{120,128}... | collective-permute-start | bytes 1376264 | tf_op jit(solution)/shard_map/ppermute | solution.py:453
  11.4 2.7 %collective-permute-start.1 = (f32[6,128,128]{2,1,0:T(8,128)S(1)}, f32[6,128,128]{2,1,0:T(8,128)S(1)}, u32[]{:S(2)}, u32[]{:S(2)}) collective-permute-start(f32[6,128,128]{2,1,0:T(8,128)S(1)} %get-tuple-element.11.down_part), channel_id=1, source_target_pairs={{8,16},{24,32},{40,48},{56,64},{72,80},{88,96},{104,112},{120,128}... | collective-permute-start | bytes 1179656 | tf_op jit(solution)/shard_map/ppermute | solution.py:455
  14.1 8.5 %collective-permute-done.1.lo_part = f32[6,128,128]{2,1,0:T(8,128)S(1)} collective-permute-done((f32[6,128,128]{2,1,0:T(8,128)S(1)}, f32[6,128,128]{2,1,0:T(8,128)S(1)}, u32[]{:S(2)}, u32[]{:S(2)}) %collective-permute-start.1) | collective-permute-done | bytes 393248 | tf_op jit(solution)/shard_map/ppermute | solution.py:455
  22.6 0.0 collective-permute-done.lo
  22.6 0.0 collective-permute-done.2.hi
  22.6 0.0 copy-done.1
  22.6 3.2 %filter.1 = f32[8,2,3,2,16,128]{5,4,3,2,1,0:T(8,128)S(1)} custom-call(f32[7,128,128]{2,1,0:T(8,128)S(1)} %collective-permute-done.lo, f32[6,128,128]{2,1,0:T(8,128)S(1)} %collective-permute-done.1.lo_part, f32[7,128,128]{2,1,0:T(8,128)S(1)} %lift.1.down, f32[6,128,128]{2,1,0:T(8,128)S(1)} %get-tuple-element.11.down_part, ...), custom_call_target="tpu_custom_call" | custom-call | tf_op jit(solution)/shard_map/filter/pallas_call | solution.py:360
  25.9 0.0 copy-start.3
  25.9 6.8 %collective-permute-start.9 = (f32[2,3,2,16,128]{4,3,2,1,0:T(8,128)S(1)}, f32[2,3,2,16,128]{4,3,2,1,0:T(8,128)S(1)}, u32[]{:S(2)}, u32[]{:S(2)}) collective-permute-start(f32[2,3,2,16,128]{4,3,2,1,0:T(8,128)S(1)} %get-tuple-element.31), channel_id=1, source_target_pairs={{0,5},{1,6},{2,7},{3,0},{4,1},{5,2},{6,3},{7,4},{8,13},{9,14},{10,... | collective-permute-start | bytes 294920 | tf_op jit(solution)/shard_map/ppermute | solution.py:430
  32.8 0.6 collective-permute-start.7
  33.4 4.5 %collective-permute-start.6 = (f32[1,3,2,16,128]{4,3,2,1,0:T(8,128)S(1)}, f32[1,3,2,16,128]{4,3,2,1,0:T(8,128)S(1)}, u32[]{:S(2)}, u32[]{:S(2)}) collective-permute-start(f32[1,3,2,16,128]{4,3,2,1,0:T(8,128)S(1)} %get-tuple-element.37), channel_id=1, source_target_pairs={{0,4},{1,5},{2,6},{3,7},{4,0},{5,1},{6,2},{7,3},{8,12},{9,13},{10,... | collective-permute-start | bytes 147464 | tf_op jit(solution)/shard_map/ppermute | solution.py:430
  37.9 1.5 %collective-permute-start.10 = (f32[2,3,2,16,128]{4,3,2,1,0:T(8,128)S(1)}, f32[2,3,2,16,128]{4,3,2,1,0:T(8,128)S(1)}, u32[]{:S(2)}, u32[]{:S(2)}) collective-permute-start(f32[2,3,2,16,128]{4,3,2,1,0:T(8,128)S(1)} %get-tuple-element.30), channel_id=1, source_target_pairs={{0,6},{1,7},{2,0},{3,1},{4,2},{5,3},{6,4},{7,5},{8,14},{9,15},{10,... | collective-permute-start | bytes 294920 | tf_op jit(solution)/shard_map/ppermute | solution.py:430
  39.3 1.0 collective-permute-start.11
  40.3 3.8 %collective-permute-done.7 = f32[1,3,2,16,128]{4,3,2,1,0:T(8,128)S(1)} collective-permute-done((f32[1,3,2,16,128]{4,3,2,1,0:T(8,128)S(1)}, f32[1,3,2,16,128]{4,3,2,1,0:T(8,128)S(1)}, u32[]{:S(2)}, u32[]{:S(2)}) %collective-permute-start.7) | collective-permute-done | bytes 49184 | tf_op jit(solution)/shard_map/ppermute | solution.py:430
  44.1 0.0 collective-permute-start.3
  44.1 0.0 collective-permute-done.6
  44.1 0.6 collective-permute-start.4
  44.7 0.0 collective-permute-done.9
  44.7 7.3 %collective-permute-start.5 = (f32[2,3,2,16,128]{4,3,2,1,0:T(8,128)S(1)}, f32[2,3,2,16,128]{4,3,2,1,0:T(8,128)S(1)}, u32[]{:S(2)}, u32[]{:S(2)}) collective-permute-start(f32[2,3,2,16,128]{4,3,2,1,0:T(8,128)S(1)} %get-tuple-element.32), channel_id=1, source_target_pairs={{0,3},{1,4},{2,5},{3,6},{4,7},{5,0},{6,1},{7,2},{8,11},{9,12},{10,... | collective-permute-start | bytes 294920 | tf_op jit(solution)/shard_map/ppermute | solution.py:430
  52.0 0.0 collective-permute-done.10
  52.0 0.6 collective-permute-start.8
  52.6 0.0 copy-done.3
  52.6 1.6 %gram.2 = (bf16[96,48,128]{2,1,0:T(8,128)(2,1)S(1)}, f32[16,32]{1,0:T(8,128)S(1)}) custom-call(f32[16,96,128]{2,1,0:T(8,128)S(1)} %bitcast.36), custom_call_target="tpu_custom_call" | custom-call | tf_op jit(solution)/shard_map/gram/pallas_call | solution.py:375
  54.2 0.0 collective-permute-done.11
  54.2 0.0 collective-permute-done.3
  54.2 0.0 collective-permute-done.4
  54.2 4.8 %collective-permute-done.5 = f32[2,3,2,16,128]{4,3,2,1,0:T(8,128)S(1)} collective-permute-done((f32[2,3,2,16,128]{4,3,2,1,0:T(8,128)S(1)}, f32[2,3,2,16,128]{4,3,2,1,0:T(8,128)S(1)}, u32[]{:S(2)}, u32[]{:S(2)}) %collective-permute-start.5) | collective-permute-done | bytes 98336 | tf_op jit(solution)/shard_map/ppermute | solution.py:430
  59.0 0.0 collective-permute-done.8
  59.0 2.1 %gram.3 = (bf16[96,48,128]{2,1,0:T(8,128)(2,1)S(1)}, f32[16,32]{1,0:T(8,128)S(1)}) custom-call(f32[2,96,128]{2,1,0:T(8,128)S(1)} %bitcast.38, f32[2,96,128]{2,1,0:T(8,128)S(1)} %bitcast.42, f32[2,96,128]{2,1,0:T(8,128)S(1)} %bitcast.43, f32[2,96,128]{2,1,0:T(8,128)S(1)} %bitcast.44, f32[1,96,128]{2,1,0:T(8,128)S(1)} %bitcast.45, f32[1,96,128]{2,1,0:T(8,128)S(1)} %bitcast.46, ...), custom_call_target="tpu_custom_call" | custom-call | tf_op jit(solution)/shard_map/gram/pallas_call | solution.py:375
  61.1 0.1 pack.1
  61.1 10.8 %all_to_all.10 = f32[16,8,128]{2,1,0:T(8,128)S(1)} all-to-all(f32[16,8,128]{2,1,0:T(8,128)S(1)} %pack.1), channel_id=1, replica_groups=mesh['x'=4,'y'=4,'core'=2,'probe'=8] {'probe','core'}, dimensions={0} | all-to-all | bytes 131072 | tf_op jit(solution)/shard_map/all_to_all | solution.py:465
  71.9 15.3 %all_to_all.11.copies = f32[16,8,128]{2,1,0:T(8,128)S(1)} all-to-all(f32[16,8,128]{2,1,0:T(8,128)S(1)} %broadcast_in_dim.2), channel_id=1, replica_groups=mesh['x'=4,'y'=4,'core'=2,'probe'=8] {'x','y'}, dimensions={0} | all-to-all | bytes 131072 | tf_op jit(solution)/shard_map/all_to_all | solution.py:467
  87.2 3.9 %finish.1 = (f32[1536,128]{1,0:T(8,128)S(1)}, f32[16,16]{1,0:T(8,128)S(1)}) custom-call(f32[16,8,128]{2,1,0:T(8,128)S(1)} %all_to_all.11.copies, bf16[96,48,128]{2,1,0:T(8,128)(2,1)S(1)} %get-tuple-element.13.refs_9_.first, bf16[96,48,128]{2,1,0:T(8,128)(2,1)S(1)} %get-tuple-element.15.second), custom_call_target="tpu_custom_call" | custom-call | tf_op jit(solution)/shard_map/finish/pallas_call | solution.py:403
  91.2 0.7 collective-permute-start.12
  92.0 1.4 %collective-permute-start.16 = (f32[1,3,2,16,128]{4,3,2,1,0:T(8,128)S(1)}, f32[1,3,2,16,128]{4,3,2,1,0:T(8,128)S(1)}, u32[]{:S(2)}, u32[]{:S(2)}) collective-permute-start(f32[1,3,2,16,128]{4,3,2,1,0:T(8,128)S(1)} %bitcast.55), channel_id=1, source_target_pairs={{0,6},{1,7},{2,0},{3,1},{4,2},{5,3},{6,4},{7,5},{8,14},{9,15},{10,... | collective-permute-start | bytes 147464 | tf_op jit(solution)/shard_map/ppermute | solution.py:430
  93.4 3.0 %collective-permute-start.15 = (f32[1,3,2,16,128]{4,3,2,1,0:T(8,128)S(1)}, f32[1,3,2,16,128]{4,3,2,1,0:T(8,128)S(1)}, u32[]{:S(2)}, u32[]{:S(2)}) collective-permute-start(f32[1,3,2,16,128]{4,3,2,1,0:T(8,128)S(1)} %bitcast.54), channel_id=1, source_target_pairs={{0,4},{1,5},{2,6},{3,7},{4,0},{5,1},{6,2},{7,3},{8,12},{9,13},{10,... | collective-permute-start | bytes 147464 | tf_op jit(solution)/shard_map/ppermute | solution.py:430
  96.4 0.6 collective-permute-start.13
  96.9 5.1 %collective-permute-start.14 = (f32[2,3,2,16,128]{4,3,2,1,0:T(8,128)S(1)}, f32[2,3,2,16,128]{4,3,2,1,0:T(8,128)S(1)}, u32[]{:S(2)}, u32[]{:S(2)}) collective-permute-start(f32[2,3,2,16,128]{4,3,2,1,0:T(8,128)S(1)} %bitcast.51), channel_id=1, source_target_pairs={{0,3},{1,4},{2,5},{3,6},{4,7},{5,0},{6,1},{7,2},{8,11},{9,12},{10,... | collective-permute-start | bytes 294920 | tf_op jit(solution)/shard_map/ppermute | solution.py:430
  102.0 0.0 collective-permute-done.16
  102.0 0.0 collective-permute-start.18
  102.0 0.0 collective-permute-done.15.refs_4_
  102.0 3.5 %collective-permute-start.19 = (f32[2,3,2,16,128]{4,3,2,1,0:T(8,128)S(1)}, f32[2,3,2,16,128]{4,3,2,1,0:T(8,128)S(1)}, u32[]{:S(2)}, u32[]{:S(2)}) collective-permute-start(f32[2,3,2,16,128]{4,3,2,1,0:T(8,128)S(1)} %bitcast.49), channel_id=1, source_target_pairs={{0,6},{1,7},{2,0},{3,1},{4,2},{5,3},{6,4},{7,5},{8,14},{9,15},{10,... | collective-permute-start | bytes 294920 | tf_op jit(solution)/shard_map/ppermute | solution.py:430
  105.5 0.0 collective-permute-done.12.refs_1_
  105.5 0.6 collective-permute-start.20
  106.2 3.1 %collective-permute-done.13.refs_2_ = f32[2,3,2,16,128]{4,3,2,1,0:T(8,128)S(1)} collective-permute-done((f32[2,3,2,16,128]{4,3,2,1,0:T(8,128)S(1)}, f32[2,3,2,16,128]{4,3,2,1,0:T(8,128)S(1)}, u32[]{:S(2)}, u32[]{:S(2)}) %collective-permute-start.13) | collective-permute-done | bytes 98336 | tf_op jit(solution)/shard_map/ppermute | solution.py:430
  109.3 0.0 collective-permute-start.17
  109.3 0.7 copy.6
  110.0 0.0 collective-permute-done.14.refs_3_
  110.0 2.6 %collective-permute-done.18.refs_6_ = f32[2,3,2,16,128]{4,3,2,1,0:T(8,128)S(1)} collective-permute-done((f32[2,3,2,16,128]{4,3,2,1,0:T(8,128)S(1)}, f32[2,3,2,16,128]{4,3,2,1,0:T(8,128)S(1)}, u32[]{:S(2)}, u32[]{:S(2)}) %collective-permute-start.18) | collective-permute-done | bytes 98336 | tf_op jit(solution)/shard_map/ppermute | solution.py:430
  112.6 2.2 %collective-permute-done.19.refs_7_ = f32[2,3,2,16,128]{4,3,2,1,0:T(8,128)S(1)} collective-permute-done((f32[2,3,2,16,128]{4,3,2,1,0:T(8,128)S(1)}, f32[2,3,2,16,128]{4,3,2,1,0:T(8,128)S(1)}, u32[]{:S(2)}, u32[]{:S(2)}) %collective-permute-start.19) | collective-permute-done | bytes 98336 | tf_op jit(solution)/shard_map/ppermute | solution.py:430
  114.8 0.9 collective-permute-done.20.refs_8_
  115.7 1.8 %collective-permute-done.17.refs_5_ = f32[1,3,2,16,128]{4,3,2,1,0:T(8,128)S(1)} collective-permute-done((f32[1,3,2,16,128]{4,3,2,1,0:T(8,128)S(1)}, f32[1,3,2,16,128]{4,3,2,1,0:T(8,128)S(1)}, u32[]{:S(2)}, u32[]{:S(2)}) %collective-permute-start.17) | collective-permute-done | bytes 49184 | tf_op jit(solution)/shard_map/ppermute | solution.py:430
  117.5 0.9 spread.1
  (6 shorter events, 0.1 us)
Async XLA Ops:
  0.6 1.1 copy-start
  1.8 1.1 copy-start.2
  2.9 0.9 copy-start.4
  3.8 18.8 %copy-start.1 = (f32[6,2,128,128]{3,2,1,0:T(8,128)S(1)}, f32[6,2,128,128]{3,2,1,0:T(8,128)}, u32[]{:S(2)}) copy-start(f32[6,2,128,128]{3,2,1,0:T(8,128)} %tangent.3) | copy-start | bytes 2359300
  5.3 17.4 %collective-permute-start.2 = (f32[13,128,128]{2,1,0:T(8,128)S(1)}, f32[13,128,128]{2,1,0:T(8,128)S(1)}, u32[]{:S(2)}, u32[]{:S(2)}) collective-permute-start(f32[13,128,128]{2,1,0:T(8,128)S(1)} %get-tuple-element.12.up), channel_id=1, source_target_pairs={{0,8},{8,0},{1,9},{9,1},{2,10},{10,2},{3,11},{11,3},{4,12},{12,4},... | collective-permute-start | bytes 2555912 | tf_op jit(solution)/shard_map/ppermute | solution.py:456
  6.4 16.2 %collective-permute-start = (f32[7,128,128]{2,1,0:T(8,128)S(1)}, f32[7,128,128]{2,1,0:T(8,128)S(1)}, u32[]{:S(2)}, u32[]{:S(2)}) collective-permute-start(f32[7,128,128]{2,1,0:T(8,128)S(1)} %lift.1.down), channel_id=1, source_target_pairs={{8,16},{24,32},{40,48},{56,64},{72,80},{88,96},{104,112},{120,128}... | collective-permute-start | bytes 1376264 | tf_op jit(solution)/shard_map/ppermute | solution.py:453
  11.4 11.2 %collective-permute-start.1 = (f32[6,128,128]{2,1,0:T(8,128)S(1)}, f32[6,128,128]{2,1,0:T(8,128)S(1)}, u32[]{:S(2)}, u32[]{:S(2)}) collective-permute-start(f32[6,128,128]{2,1,0:T(8,128)S(1)} %get-tuple-element.11.down_part), channel_id=1, source_target_pairs={{8,16},{24,32},{40,48},{56,64},{72,80},{88,96},{104,112},{120,128}... | collective-permute-start | bytes 1179656 | tf_op jit(solution)/shard_map/ppermute | solution.py:455
  25.9 26.7 %copy-start.3 = (f32[16,3,2,16,128]{4,3,2,1,0:T(8,128)S(1)}, f32[16,3,2,16,128]{4,3,2,1,0:T(8,128)}, u32[]{:S(2)}) copy-start(f32[16,3,2,16,128]{4,3,2,1,0:T(8,128)} %param.5) | copy-start | bytes 2359300
  25.9 18.8 %collective-permute-start.9 = (f32[2,3,2,16,128]{4,3,2,1,0:T(8,128)S(1)}, f32[2,3,2,16,128]{4,3,2,1,0:T(8,128)S(1)}, u32[]{:S(2)}, u32[]{:S(2)}) collective-permute-start(f32[2,3,2,16,128]{4,3,2,1,0:T(8,128)S(1)} %get-tuple-element.31), channel_id=1, source_target_pairs={{0,5},{1,6},{2,7},{3,0},{4,1},{5,2},{6,3},{7,4},{8,13},{9,14},{10,... | collective-permute-start | bytes 294920 | tf_op jit(solution)/shard_map/ppermute | solution.py:430
  32.8 11.3 %collective-permute-start.7 = (f32[1,3,2,16,128]{4,3,2,1,0:T(8,128)S(1)}, f32[1,3,2,16,128]{4,3,2,1,0:T(8,128)S(1)}, u32[]{:S(2)}, u32[]{:S(2)}) collective-permute-start(f32[1,3,2,16,128]{4,3,2,1,0:T(8,128)S(1)} %get-tuple-element.36), channel_id=1, source_target_pairs={{0,6},{1,7},{2,0},{3,1},{4,2},{5,3},{6,4},{7,5},{8,14},{9,15},{10,... | collective-permute-start | bytes 147464 | tf_op jit(solution)/shard_map/ppermute | solution.py:430
  33.4 10.7 %collective-permute-start.6 = (f32[1,3,2,16,128]{4,3,2,1,0:T(8,128)S(1)}, f32[1,3,2,16,128]{4,3,2,1,0:T(8,128)S(1)}, u32[]{:S(2)}, u32[]{:S(2)}) collective-permute-start(f32[1,3,2,16,128]{4,3,2,1,0:T(8,128)S(1)} %get-tuple-element.37), channel_id=1, source_target_pairs={{0,4},{1,5},{2,6},{3,7},{4,0},{5,1},{6,2},{7,3},{8,12},{9,13},{10,... | collective-permute-start | bytes 147464 | tf_op jit(solution)/shard_map/ppermute | solution.py:430
  37.9 14.1 %collective-permute-start.10 = (f32[2,3,2,16,128]{4,3,2,1,0:T(8,128)S(1)}, f32[2,3,2,16,128]{4,3,2,1,0:T(8,128)S(1)}, u32[]{:S(2)}, u32[]{:S(2)}) collective-permute-start(f32[2,3,2,16,128]{4,3,2,1,0:T(8,128)S(1)} %get-tuple-element.30), channel_id=1, source_target_pairs={{0,6},{1,7},{2,0},{3,1},{4,2},{5,3},{6,4},{7,5},{8,14},{9,15},{10,... | collective-permute-start | bytes 294920 | tf_op jit(solution)/shard_map/ppermute | solution.py:430
  39.3 14.9 %collective-permute-start.11 = (f32[2,3,2,16,128]{4,3,2,1,0:T(8,128)S(1)}, f32[2,3,2,16,128]{4,3,2,1,0:T(8,128)S(1)}, u32[]{:S(2)}, u32[]{:S(2)}) collective-permute-start(f32[2,3,2,16,128]{4,3,2,1,0:T(8,128)S(1)} %get-tuple-element.29), channel_id=1, source_target_pairs={{0,7},{1,0},{2,1},{3,2},{4,3},{5,4},{6,5},{7,6},{8,15},{9,8},{10,9... | collective-permute-start | bytes 294920 | tf_op jit(solution)/shard_map/ppermute | solution.py:430
  44.1 10.1 %collective-permute-start.3 = (f32[2,3,2,16,128]{4,3,2,1,0:T(8,128)S(1)}, f32[2,3,2,16,128]{4,3,2,1,0:T(8,128)S(1)}, u32[]{:S(2)}, u32[]{:S(2)}) collective-permute-start(f32[2,3,2,16,128]{4,3,2,1,0:T(8,128)S(1)} %get-tuple-element.34), channel_id=1, source_target_pairs={{0,1},{1,2},{2,3},{3,4},{4,5},{5,6},{6,7},{7,0},{8,9},{9,10},{10,1... | collective-permute-start | bytes 294920 | tf_op jit(solution)/shard_map/ppermute | solution.py:430
  44.1 10.1 %collective-permute-start.4 = (f32[2,3,2,16,128]{4,3,2,1,0:T(8,128)S(1)}, f32[2,3,2,16,128]{4,3,2,1,0:T(8,128)S(1)}, u32[]{:S(2)}, u32[]{:S(2)}) collective-permute-start(f32[2,3,2,16,128]{4,3,2,1,0:T(8,128)S(1)} %get-tuple-element.33), channel_id=1, source_target_pairs={{0,2},{1,3},{2,4},{3,5},{4,6},{5,7},{6,0},{7,1},{8,10},{9,11},{10,... | collective-permute-start | bytes 294920 | tf_op jit(solution)/shard_map/ppermute | solution.py:430
  44.7 14.3 %collective-permute-start.5 = (f32[2,3,2,16,128]{4,3,2,1,0:T(8,128)S(1)}, f32[2,3,2,16,128]{4,3,2,1,0:T(8,128)S(1)}, u32[]{:S(2)}, u32[]{:S(2)}) collective-permute-start(f32[2,3,2,16,128]{4,3,2,1,0:T(8,128)S(1)} %get-tuple-element.32), channel_id=1, source_target_pairs={{0,3},{1,4},{2,5},{3,6},{4,7},{5,0},{6,1},{7,2},{8,11},{9,12},{10,... | collective-permute-start | bytes 294920 | tf_op jit(solution)/shard_map/ppermute | solution.py:430
  52.0 7.0 %collective-permute-start.8 = (f32[1,3,2,16,128]{4,3,2,1,0:T(8,128)S(1)}, f32[1,3,2,16,128]{4,3,2,1,0:T(8,128)S(1)}, u32[]{:S(2)}, u32[]{:S(2)}) collective-permute-start(f32[1,3,2,16,128]{4,3,2,1,0:T(8,128)S(1)} %collective-permute-done.7), channel_id=1, source_target_pairs={{0,6},{1,7},{2,0},{3,1},{4,2},{5,3},{6,4},{7,5},{8,14},{9,15},{10,... | collective-permute-start | bytes 147464 | tf_op jit(solution)/shard_map/ppermute | solution.py:430
  91.2 14.3 %collective-permute-start.12 = (f32[2,3,2,16,128]{4,3,2,1,0:T(8,128)S(1)}, f32[2,3,2,16,128]{4,3,2,1,0:T(8,128)S(1)}, u32[]{:S(2)}, u32[]{:S(2)}) collective-permute-start(f32[2,3,2,16,128]{4,3,2,1,0:T(8,128)S(1)} %bitcast.53), channel_id=1, source_target_pairs={{0,1},{1,2},{2,3},{3,4},{4,5},{5,6},{6,7},{7,0},{8,9},{9,10},{10,1... | collective-permute-start | bytes 294920 | tf_op jit(solution)/shard_map/ppermute | solution.py:430
  92.0 10.1 %collective-permute-start.16 = (f32[1,3,2,16,128]{4,3,2,1,0:T(8,128)S(1)}, f32[1,3,2,16,128]{4,3,2,1,0:T(8,128)S(1)}, u32[]{:S(2)}, u32[]{:S(2)}) collective-permute-start(f32[1,3,2,16,128]{4,3,2,1,0:T(8,128)S(1)} %bitcast.55), channel_id=1, source_target_pairs={{0,6},{1,7},{2,0},{3,1},{4,2},{5,3},{6,4},{7,5},{8,14},{9,15},{10,... | collective-permute-start | bytes 147464 | tf_op jit(solution)/shard_map/ppermute | solution.py:430
  93.4 8.7 %collective-permute-start.15 = (f32[1,3,2,16,128]{4,3,2,1,0:T(8,128)S(1)}, f32[1,3,2,16,128]{4,3,2,1,0:T(8,128)S(1)}, u32[]{:S(2)}, u32[]{:S(2)}) collective-permute-start(f32[1,3,2,16,128]{4,3,2,1,0:T(8,128)S(1)} %bitcast.54), channel_id=1, source_target_pairs={{0,4},{1,5},{2,6},{3,7},{4,0},{5,1},{6,2},{7,3},{8,12},{9,13},{10,... | collective-permute-start | bytes 147464 | tf_op jit(solution)/shard_map/ppermute | solution.py:430
  96.4 12.9 %collective-permute-start.13 = (f32[2,3,2,16,128]{4,3,2,1,0:T(8,128)S(1)}, f32[2,3,2,16,128]{4,3,2,1,0:T(8,128)S(1)}, u32[]{:S(2)}, u32[]{:S(2)}) collective-permute-start(f32[2,3,2,16,128]{4,3,2,1,0:T(8,128)S(1)} %bitcast.52), channel_id=1, source_target_pairs={{0,2},{1,3},{2,4},{3,5},{4,6},{5,7},{6,0},{7,1},{8,10},{9,11},{10,... | collective-permute-start | bytes 294920 | tf_op jit(solution)/shard_map/ppermute | solution.py:430
  96.9 13.0 %collective-permute-start.14 = (f32[2,3,2,16,128]{4,3,2,1,0:T(8,128)S(1)}, f32[2,3,2,16,128]{4,3,2,1,0:T(8,128)S(1)}, u32[]{:S(2)}, u32[]{:S(2)}) collective-permute-start(f32[2,3,2,16,128]{4,3,2,1,0:T(8,128)S(1)} %bitcast.51), channel_id=1, source_target_pairs={{0,3},{1,4},{2,5},{3,6},{4,7},{5,0},{6,1},{7,2},{8,11},{9,12},{10,... | collective-permute-start | bytes 294920 | tf_op jit(solution)/shard_map/ppermute | solution.py:430
  102.0 10.5 %collective-permute-start.18 = (f32[2,3,2,16,128]{4,3,2,1,0:T(8,128)S(1)}, f32[2,3,2,16,128]{4,3,2,1,0:T(8,128)S(1)}, u32[]{:S(2)}, u32[]{:S(2)}) collective-permute-start(f32[2,3,2,16,128]{4,3,2,1,0:T(8,128)S(1)} %bitcast.50), channel_id=1, source_target_pairs={{0,5},{1,6},{2,7},{3,0},{4,1},{5,2},{6,3},{7,4},{8,13},{9,14},{10,... | collective-permute-start | bytes 294920 | tf_op jit(solution)/shard_map/ppermute | solution.py:430
  102.0 12.8 %collective-permute-start.19 = (f32[2,3,2,16,128]{4,3,2,1,0:T(8,128)S(1)}, f32[2,3,2,16,128]{4,3,2,1,0:T(8,128)S(1)}, u32[]{:S(2)}, u32[]{:S(2)}) collective-permute-start(f32[2,3,2,16,128]{4,3,2,1,0:T(8,128)S(1)} %bitcast.49), channel_id=1, source_target_pairs={{0,6},{1,7},{2,0},{3,1},{4,2},{5,3},{6,4},{7,5},{8,14},{9,15},{10,... | collective-permute-start | bytes 294920 | tf_op jit(solution)/shard_map/ppermute | solution.py:430
  105.5 10.2 %collective-permute-start.20 = (f32[2,3,2,16,128]{4,3,2,1,0:T(8,128)S(1)}, f32[2,3,2,16,128]{4,3,2,1,0:T(8,128)S(1)}, u32[]{:S(2)}, u32[]{:S(2)}) collective-permute-start(f32[2,3,2,16,128]{4,3,2,1,0:T(8,128)S(1)} %bitcast.48), channel_id=1, source_target_pairs={{0,7},{1,0},{2,1},{3,2},{4,3},{5,4},{6,5},{7,6},{8,15},{9,8},{10,9... | collective-permute-start | bytes 294920 | tf_op jit(solution)/shard_map/ppermute | solution.py:430
  109.3 8.3 %collective-permute-start.17 = (f32[1,3,2,16,128]{4,3,2,1,0:T(8,128)S(1)}, f32[1,3,2,16,128]{4,3,2,1,0:T(8,128)S(1)}, u32[]{:S(2)}, u32[]{:S(2)}) collective-permute-start(f32[1,3,2,16,128]{4,3,2,1,0:T(8,128)S(1)} %collective-permute-done.16), channel_id=1, source_target_pairs={{0,6},{1,7},{2,0},{3,1},{4,2},{5,3},{6,4},{7,5},{8,14},{9,15},{10,... | collective-permute-start | bytes 147464 | tf_op jit(solution)/shard_map/ppermute | solution.py:430

commit v2 on v1

--- a/solution.py
+++ b/solution.py
@@ -57,13 +57,14 @@
     )
 
 
-def lift_kernel(probes_far, modulus_far, out, sems):
+def lift_kernel(probes_far, modulus_far, tangent_far, out, tangent, sems):
     count = probes_far.shape[0]
     core = lax.axis_index("core")
     copies = [
         pltpu.make_async_copy(probes_far.at[k, :, core], out.at[pl.ds(3 * k, 3)], sems.at[k]) for k in range(count)
     ]
     copies.append(pltpu.make_async_copy(modulus_far.at[pl.ds(core, 1)], out.at[pl.ds(3 * count, 1)], sems.at[count]))
+    copies.append(pltpu.make_async_copy(tangent_far, tangent, sems.at[count + 1]))
     for copy in copies:
         copy.start()
     for copy in copies:
@@ -326,17 +327,20 @@
     return tuple(pltpu.with_memory_space_constraint(a, pltpu.HBM) for a in arrays)
 
 
-def lift_call(probes, modulus):
+def lift_call(probes, modulus, tangent):
     count, _, _, height, breadth = probes.shape
     return pl.pallas_call(
         lift_kernel,
-        out_shape=pltpu.VMEM((3 * count + 1, height, breadth), jnp.float32),
-        in_specs=[FAR, FAR],
-        out_specs=VM,
-        scratch_shapes=[pltpu.SemaphoreType.DMA((count + 1,))],
+        out_shape=(
+            pltpu.VMEM((3 * count + 1, height, breadth), jnp.float32),
+            pltpu.VMEM(tangent.shape, jnp.float32),
+        ),
+        in_specs=[FAR] * 3,
+        out_specs=(VM, VM),
+        scratch_shapes=[pltpu.SemaphoreType.DMA((count + 2,))],
         compiler_params=pltpu.CompilerParams(vmem_limit_bytes=1 << 20),
         name="lift",
-    )(*in_far(probes, modulus))
+    )(*in_far(probes, modulus, tangent))
 
 
 def partial_call(probes, modulus, tangent):
@@ -449,13 +453,13 @@
     length = math.prod(earlier.shape[1:-1])
     places = ("x", "y", "core")
     outer = [(i, i + 1) for i in range(1, slabs - 1, 2)] + [(i, i - 1) for i in range(2, slabs, 2)]
-    raw = lift_call(probes, modulus)
+    raw, tensor = lift_call(probes, modulus, tangent)
     got_raw = lax.ppermute(raw, places, outer)
-    far, near = partial_call(probes, modulus, tangent)
+    far, near = partial_call(probes, modulus, tensor)
     got_far = lax.ppermute(far, places, outer)
     got_near = lax.ppermute(near, "core", [(0, 1), (1, 0)])
     first, first_gram = gram_call([earlier.reshape(kept, length, breadth)], ((0, 0),))
-    filtered = filter_call((got_raw, got_far, raw, far, near, got_near), tangent)
+    filtered = filter_call((got_raw, got_far, raw, far, near, got_near), tensor)
     got = exchange([filtered[k] for k in range(columns)], columns)
     half = columns // 2
     pieces = [(k, 0) for k in range(half + 1)] + [(half, 1)] + [(k, 0) for k in range(half + 1, columns)]

time: 119 us -> 117 us (0.983)
  local copies, waits for them, and re-layouts: 3.96 us -> 0.89 us
    unnamed x11 -> x7, local copies, waits for them, and re-layouts: 3.84 us -> 0.77 us
  transfers between devices with their start and end apart: 21 -> 21, of which waited for: 8 -> 8; matrix products, arithmetic and copies ran while one was open for 1% -> 1% of each run, Pallas kernels for 2% -> 1%
where the time goes in v2:
time: 117 us; the launch traced here: 116 us
  starting transfers between devices  45.6 us (39%)
  waiting for transfers between devices  27.7 us (24%)
  blocking collectives  26.1 us (22%)
  Pallas kernels  14.8 us (13%)
    ppermute x18, starting transfers between devices, shift(): lax.ppermute(block, 'probe', [(j, (j + by) % columns) for j in range(colu...  37.8 us
    ppermute x18, waiting for transfers between devices, shift(): lax.ppermute(block, 'probe', [(j, (j + by) % columns) for j in range(colu...  19.2 us
    all_to_all x1, blocking collectives, body(): copies = lax.all_to_all(copies, ('x', 'y'), 0, 0, tiled=True)  15.3 us
    all_to_all x1, blocking collectives, body(): copies = lax.all_to_all(copies, ('probe', 'core'), 0, 0, tiled=True)  10.8 us
    ppermute x1, waiting for transfers between devices, body(): got_far = lax.ppermute(far, places, outer)  8.51 us
    ppermute x1, starting transfers between devices, body(): got_raw = lax.ppermute(raw, places, outer)  4.98 us
    pallas_call x1, Pallas kernels, finish_call(): pl.pallas_call(functools.partial(finish_kernel, factor=scale), out_shape=...  3.93 us
    pallas_call x2, Pallas kernels, gram_call(): pl.pallas_call(functools.partial(gram_kernel, pieces=pieces, alone=alone)...  3.69 us
  transfers between devices with their start and end apart: 21, of which 8 were waited for; matrix products, arithmetic and copies ran while one was open for 1% of the time, Pallas kernels for 1%

profile of v2, /device:TPU:2, one launch (start us, length us, event | category | flops | bytes accessed | tf_op | source)
XLA Modules:
  0.0 116.0 jit_solution(6906736403641799458)
XLA Ops:
  0.6 0.0 copy-start
  0.6 0.0 copy-start.2
  0.6 1.5 %lift.1 = (f32[7,128,128]{2,1,0:T(8,128)S(1)}, f32[6,2,128,128]{3,2,1,0:T(8,128)S(1)}) custom-call(f32[2,3,2,128,128]{4,3,2,1,0:T(8,128)} %probes.1, f32[2,128,128]{2,1,0:T(8,128)} %modulus.1, f32[6,2,128,128]{3,2,1,0:T(8,128)} %tangent_far.1), custom_call_target="tpu_custom_call" | custom-call | tf_op jit(solution)/shard_map/lift/pallas_call | solution.py:332
  2.1 0.1 copy-done
  2.2 0.0 copy-done.2
  2.2 1.5 %partial.1 = (f32[6,128,128]{2,1,0:T(8,128)S(1)}, f32[13,128,128]{2,1,0:T(8,128)S(1)}) custom-call(f32[2,3,2,128,128]{4,3,2,1,0:T(8,128)S(1)} %copy-done, f32[2,128,128]{2,1,0:T(8,128)S(1)} %copy-done.2, f32[6,2,128,128]{3,2,1,0:T(8,128)S(1)} %get-tuple-element.14.tangent), custom_call_target="tpu_custom_call" | custom-call | tf_op jit(solution)/shard_map/partial/pallas_call | solution.py:349
  3.7 0.1 collective-permute-start.2
  3.8 5.0 %collective-permute-start = (f32[7,128,128]{2,1,0:T(8,128)S(1)}, f32[7,128,128]{2,1,0:T(8,128)S(1)}, u32[]{:S(2)}, u32[]{:S(2)}) collective-permute-start(f32[7,128,128]{2,1,0:T(8,128)S(1)} %get-tuple-element.13.down), channel_id=1, source_target_pairs={{8,16},{24,32},{40,48},{56,64},{72,80},{88,96},{104,112},{120,128}... | collective-permute-start | bytes 1376264 | tf_op jit(solution)/shard_map/ppermute | solution.py:457
  8.8 2.7 %collective-permute-start.1 = (f32[6,128,128]{2,1,0:T(8,128)S(1)}, f32[6,128,128]{2,1,0:T(8,128)S(1)}, u32[]{:S(2)}, u32[]{:S(2)}) collective-permute-start(f32[6,128,128]{2,1,0:T(8,128)S(1)} %get-tuple-element.15.down_part), channel_id=1, source_target_pairs={{8,16},{24,32},{40,48},{56,64},{72,80},{88,96},{104,112},{120,128}... | collective-permute-start | bytes 1179656 | tf_op jit(solution)/shard_map/ppermute | solution.py:459
  11.5 8.5 %collective-permute-done.1.lo_part = f32[6,128,128]{2,1,0:T(8,128)S(1)} collective-permute-done((f32[6,128,128]{2,1,0:T(8,128)S(1)}, f32[6,128,128]{2,1,0:T(8,128)S(1)}, u32[]{:S(2)}, u32[]{:S(2)}) %collective-permute-start.1) | collective-permute-done | bytes 393248 | tf_op jit(solution)/shard_map/ppermute | solution.py:459
  20.0 0.0 collective-permute-done.lo
  20.0 0.0 collective-permute-done.2.hi
  20.0 3.2 %filter.1 = f32[8,2,3,2,16,128]{5,4,3,2,1,0:T(8,128)S(1)} custom-call(f32[7,128,128]{2,1,0:T(8,128)S(1)} %collective-permute-done.lo, f32[6,128,128]{2,1,0:T(8,128)S(1)} %collective-permute-done.1.lo_part, f32[7,128,128]{2,1,0:T(8,128)S(1)} %get-tuple-element.13.down, f32[6,128,128]{2,1,0:T(8,128)S(1)} %get-tuple-element.15.down_part, ...), custom_call_target="tpu_custom_call" | custom-call | tf_op jit(solution)/shard_map/filter/pallas_call | solution.py:364
  23.2 0.0 copy-start.1
  23.3 6.8 %collective-permute-start.9 = (f32[2,3,2,16,128]{4,3,2,1,0:T(8,128)S(1)}, f32[2,3,2,16,128]{4,3,2,1,0:T(8,128)S(1)}, u32[]{:S(2)}, u32[]{:S(2)}) collective-permute-start(f32[2,3,2,16,128]{4,3,2,1,0:T(8,128)S(1)} %get-tuple-element.35), channel_id=1, source_target_pairs={{0,5},{1,6},{2,7},{3,0},{4,1},{5,2},{6,3},{7,4},{8,13},{9,14},{10,... | collective-permute-start | bytes 294920 | tf_op jit(solution)/shard_map/ppermute | solution.py:434
  30.1 0.6 collective-permute-start.7
  30.7 4.5 %collective-permute-start.6 = (f32[1,3,2,16,128]{4,3,2,1,0:T(8,128)S(1)}, f32[1,3,2,16,128]{4,3,2,1,0:T(8,128)S(1)}, u32[]{:S(2)}, u32[]{:S(2)}) collective-permute-start(f32[1,3,2,16,128]{4,3,2,1,0:T(8,128)S(1)} %get-tuple-element.41), channel_id=1, source_target_pairs={{0,4},{1,5},{2,6},{3,7},{4,0},{5,1},{6,2},{7,3},{8,12},{9,13},{10,... | collective-permute-start | bytes 147464 | tf_op jit(solution)/shard_map/ppermute | solution.py:434
  35.2 1.5 %collective-permute-start.10 = (f32[2,3,2,16,128]{4,3,2,1,0:T(8,128)S(1)}, f32[2,3,2,16,128]{4,3,2,1,0:T(8,128)S(1)}, u32[]{:S(2)}, u32[]{:S(2)}) collective-permute-start(f32[2,3,2,16,128]{4,3,2,1,0:T(8,128)S(1)} %get-tuple-element.34), channel_id=1, source_target_pairs={{0,6},{1,7},{2,0},{3,1},{4,2},{5,3},{6,4},{7,5},{8,14},{9,15},{10,... | collective-permute-start | bytes 294920 | tf_op jit(solution)/shard_map/ppermute | solution.py:434
  36.7 1.0 collective-permute-start.11
  37.7 3.8 %collective-permute-done.7 = f32[1,3,2,16,128]{4,3,2,1,0:T(8,128)S(1)} collective-permute-done((f32[1,3,2,16,128]{4,3,2,1,0:T(8,128)S(1)}, f32[1,3,2,16,128]{4,3,2,1,0:T(8,128)S(1)}, u32[]{:S(2)}, u32[]{:S(2)}) %collective-permute-start.7) | collective-permute-done | bytes 49184 | tf_op jit(solution)/shard_map/ppermute | solution.py:434
  41.4 0.0 collective-permute-start.3
  41.4 0.0 collective-permute-done.6
  41.4 0.6 collective-permute-start.4
  42.1 0.0 collective-permute-done.9
  42.1 7.3 %collective-permute-start.5 = (f32[2,3,2,16,128]{4,3,2,1,0:T(8,128)S(1)}, f32[2,3,2,16,128]{4,3,2,1,0:T(8,128)S(1)}, u32[]{:S(2)}, u32[]{:S(2)}) collective-permute-start(f32[2,3,2,16,128]{4,3,2,1,0:T(8,128)S(1)} %get-tuple-element.36), channel_id=1, source_target_pairs={{0,3},{1,4},{2,5},{3,6},{4,7},{5,0},{6,1},{7,2},{8,11},{9,12},{10,... | collective-permute-start | bytes 294920 | tf_op jit(solution)/shard_map/ppermute | solution.py:434
  49.3 0.0 collective-permute-done.10
  49.3 0.6 collective-permute-start.8
  49.9 0.0 copy-done.1
  49.9 1.6 %gram.2 = (bf16[96,48,128]{2,1,0:T(8,128)(2,1)S(1)}, f32[16,32]{1,0:T(8,128)S(1)}) custom-call(f32[16,96,128]{2,1,0:T(8,128)S(1)} %bitcast.36), custom_call_target="tpu_custom_call" | custom-call | tf_op jit(solution)/shard_map/gram/pallas_call | solution.py:379
  51.6 0.0 collective-permute-done.11
  51.6 0.0 collective-permute-done.3
  51.6 0.0 collective-permute-done.4
  51.6 4.8 %collective-permute-done.5 = f32[2,3,2,16,128]{4,3,2,1,0:T(8,128)S(1)} collective-permute-done((f32[2,3,2,16,128]{4,3,2,1,0:T(8,128)S(1)}, f32[2,3,2,16,128]{4,3,2,1,0:T(8,128)S(1)}, u32[]{:S(2)}, u32[]{:S(2)}) %collective-permute-start.5) | collective-permute-done | bytes 98336 | tf_op jit(solution)/shard_map/ppermute | solution.py:434
  56.3 0.0 collective-permute-done.8
  56.3 2.1 %gram.3 = (bf16[96,48,128]{2,1,0:T(8,128)(2,1)S(1)}, f32[16,32]{1,0:T(8,128)S(1)}) custom-call(f32[2,96,128]{2,1,0:T(8,128)S(1)} %bitcast.38, f32[2,96,128]{2,1,0:T(8,128)S(1)} %bitcast.42, f32[2,96,128]{2,1,0:T(8,128)S(1)} %bitcast.43, f32[2,96,128]{2,1,0:T(8,128)S(1)} %bitcast.44, f32[1,96,128]{2,1,0:T(8,128)S(1)} %bitcast.45, f32[1,96,128]{2,1,0:T(8,128)S(1)} %bitcast.46, ...), custom_call_target="tpu_custom_call" | custom-call | tf_op jit(solution)/shard_map/gram/pallas_call | solution.py:379
  58.4 0.1 pack.1
  58.5 10.8 %all_to_all.10 = f32[16,8,128]{2,1,0:T(8,128)S(1)} all-to-all(f32[16,8,128]{2,1,0:T(8,128)S(1)} %pack.1), channel_id=1, replica_groups=mesh['x'=4,'y'=4,'core'=2,'probe'=8] {'probe','core'}, dimensions={0} | all-to-all | bytes 131072 | tf_op jit(solution)/shard_map/all_to_all | solution.py:469
  69.3 15.3 %all_to_all.11.copies = f32[16,8,128]{2,1,0:T(8,128)S(1)} all-to-all(f32[16,8,128]{2,1,0:T(8,128)S(1)} %broadcast_in_dim.2), channel_id=1, replica_groups=mesh['x'=4,'y'=4,'core'=2,'probe'=8] {'x','y'}, dimensions={0} | all-to-all | bytes 131072 | tf_op jit(solution)/shard_map/all_to_all | solution.py:471
  84.6 3.9 %finish.1 = (f32[1536,128]{1,0:T(8,128)S(1)}, f32[16,16]{1,0:T(8,128)S(1)}) custom-call(f32[16,8,128]{2,1,0:T(8,128)S(1)} %all_to_all.11.copies, bf16[96,48,128]{2,1,0:T(8,128)(2,1)S(1)} %get-tuple-element.17.refs_9_.first, bf16[96,48,128]{2,1,0:T(8,128)(2,1)S(1)} %get-tuple-element.19.second), custom_call_target="tpu_custom_call" | custom-call | tf_op jit(solution)/shard_map/finish/pallas_call | solution.py:407
  88.6 0.7 collective-permute-start.12
  89.3 1.4 %collective-permute-start.16 = (f32[1,3,2,16,128]{4,3,2,1,0:T(8,128)S(1)}, f32[1,3,2,16,128]{4,3,2,1,0:T(8,128)S(1)}, u32[]{:S(2)}, u32[]{:S(2)}) collective-permute-start(f32[1,3,2,16,128]{4,3,2,1,0:T(8,128)S(1)} %bitcast.55), channel_id=1, source_target_pairs={{0,6},{1,7},{2,0},{3,1},{4,2},{5,3},{6,4},{7,5},{8,14},{9,15},{10,... | collective-permute-start | bytes 147464 | tf_op jit(solution)/shard_map/ppermute | solution.py:434
  90.7 3.0 %collective-permute-start.15 = (f32[1,3,2,16,128]{4,3,2,1,0:T(8,128)S(1)}, f32[1,3,2,16,128]{4,3,2,1,0:T(8,128)S(1)}, u32[]{:S(2)}, u32[]{:S(2)}) collective-permute-start(f32[1,3,2,16,128]{4,3,2,1,0:T(8,128)S(1)} %bitcast.54), channel_id=1, source_target_pairs={{0,4},{1,5},{2,6},{3,7},{4,0},{5,1},{6,2},{7,3},{8,12},{9,13},{10,... | collective-permute-start | bytes 147464 | tf_op jit(solution)/shard_map/ppermute | solution.py:434
  93.7 0.6 collective-permute-start.13
  94.3 5.1 %collective-permute-start.14 = (f32[2,3,2,16,128]{4,3,2,1,0:T(8,128)S(1)}, f32[2,3,2,16,128]{4,3,2,1,0:T(8,128)S(1)}, u32[]{:S(2)}, u32[]{:S(2)}) collective-permute-start(f32[2,3,2,16,128]{4,3,2,1,0:T(8,128)S(1)} %bitcast.51), channel_id=1, source_target_pairs={{0,3},{1,4},{2,5},{3,6},{4,7},{5,0},{6,1},{7,2},{8,11},{9,12},{10,... | collective-permute-start | bytes 294920 | tf_op jit(solution)/shard_map/ppermute | solution.py:434
  99.4 0.0 collective-permute-done.16
  99.4 0.0 collective-permute-start.18
  99.4 0.0 collective-permute-done.15.refs_4_
  99.4 3.5 %collective-permute-start.19 = (f32[2,3,2,16,128]{4,3,2,1,0:T(8,128)S(1)}, f32[2,3,2,16,128]{4,3,2,1,0:T(8,128)S(1)}, u32[]{:S(2)}, u32[]{:S(2)}) collective-permute-start(f32[2,3,2,16,128]{4,3,2,1,0:T(8,128)S(1)} %bitcast.49), channel_id=1, source_target_pairs={{0,6},{1,7},{2,0},{3,1},{4,2},{5,3},{6,4},{7,5},{8,14},{9,15},{10,... | collective-permute-start | bytes 294920 | tf_op jit(solution)/shard_map/ppermute | solution.py:434
  102.9 0.0 collective-permute-done.12.refs_1_
  102.9 0.6 collective-permute-start.20
  103.5 3.1 %collective-permute-done.13.refs_2_ = f32[2,3,2,16,128]{4,3,2,1,0:T(8,128)S(1)} collective-permute-done((f32[2,3,2,16,128]{4,3,2,1,0:T(8,128)S(1)}, f32[2,3,2,16,128]{4,3,2,1,0:T(8,128)S(1)}, u32[]{:S(2)}, u32[]{:S(2)}) %collective-permute-start.13) | collective-permute-done | bytes 98336 | tf_op jit(solution)/shard_map/ppermute | solution.py:434
  106.6 0.0 collective-permute-start.17
  106.6 0.7 copy.6
  107.3 0.0 collective-permute-done.14.refs_3_
  107.3 2.6 %collective-permute-done.18.refs_6_ = f32[2,3,2,16,128]{4,3,2,1,0:T(8,128)S(1)} collective-permute-done((f32[2,3,2,16,128]{4,3,2,1,0:T(8,128)S(1)}, f32[2,3,2,16,128]{4,3,2,1,0:T(8,128)S(1)}, u32[]{:S(2)}, u32[]{:S(2)}) %collective-permute-start.18) | collective-permute-done | bytes 98336 | tf_op jit(solution)/shard_map/ppermute | solution.py:434
  109.9 2.2 %collective-permute-done.19.refs_7_ = f32[2,3,2,16,128]{4,3,2,1,0:T(8,128)S(1)} collective-permute-done((f32[2,3,2,16,128]{4,3,2,1,0:T(8,128)S(1)}, f32[2,3,2,16,128]{4,3,2,1,0:T(8,128)S(1)}, u32[]{:S(2)}, u32[]{:S(2)}) %collective-permute-start.19) | collective-permute-done | bytes 98336 | tf_op jit(solution)/shard_map/ppermute | solution.py:434
  112.2 0.9 collective-permute-done.20.refs_8_
  113.1 1.8 %collective-permute-done.17.refs_5_ = f32[1,3,2,16,128]{4,3,2,1,0:T(8,128)S(1)} collective-permute-done((f32[1,3,2,16,128]{4,3,2,1,0:T(8,128)S(1)}, f32[1,3,2,16,128]{4,3,2,1,0:T(8,128)S(1)}, u32[]{:S(2)}, u32[]{:S(2)}) %collective-permute-start.17) | collective-permute-done | bytes 49184 | tf_op jit(solution)/shard_map/ppermute | solution.py:434
  114.9 0.9 spread.1
  (6 shorter events, 0.1 us)
Async XLA Ops:
  0.6 1.6 %copy-start = (f32[2,3,2,128,128]{4,3,2,1,0:T(8,128)S(1)}, f32[2,3,2,128,128]{4,3,2,1,0:T(8,128)}, u32[]{:S(2)}) copy-start(f32[2,3,2,128,128]{4,3,2,1,0:T(8,128)} %probes.1) | copy-start | bytes 2359300
  0.6 1.6 %copy-start.2 = (f32[2,128,128]{2,1,0:T(8,128)S(1)}, f32[2,128,128]{2,1,0:T(8,128)}, u32[]{:S(2)}) copy-start(f32[2,128,128]{2,1,0:T(8,128)} %modulus.1) | copy-start | bytes 393220
  3.7 16.3 %collective-permute-start.2 = (f32[13,128,128]{2,1,0:T(8,128)S(1)}, f32[13,128,128]{2,1,0:T(8,128)S(1)}, u32[]{:S(2)}, u32[]{:S(2)}) collective-permute-start(f32[13,128,128]{2,1,0:T(8,128)S(1)} %get-tuple-element.16.up), channel_id=1, source_target_pairs={{0,8},{8,0},{1,9},{9,1},{2,10},{10,2},{3,11},{11,3},{4,12},{12,4},... | collective-permute-start | bytes 2555912 | tf_op jit(solution)/shard_map/ppermute | solution.py:460
  3.8 16.2 %collective-permute-start = (f32[7,128,128]{2,1,0:T(8,128)S(1)}, f32[7,128,128]{2,1,0:T(8,128)S(1)}, u32[]{:S(2)}, u32[]{:S(2)}) collective-permute-start(f32[7,128,128]{2,1,0:T(8,128)S(1)} %get-tuple-element.13.down), channel_id=1, source_target_pairs={{8,16},{24,32},{40,48},{56,64},{72,80},{88,96},{104,112},{120,128}... | collective-permute-start | bytes 1376264 | tf_op jit(solution)/shard_map/ppermute | solution.py:457
  8.8 11.2 %collective-permute-start.1 = (f32[6,128,128]{2,1,0:T(8,128)S(1)}, f32[6,128,128]{2,1,0:T(8,128)S(1)}, u32[]{:S(2)}, u32[]{:S(2)}) collective-permute-start(f32[6,128,128]{2,1,0:T(8,128)S(1)} %get-tuple-element.15.down_part), channel_id=1, source_target_pairs={{8,16},{24,32},{40,48},{56,64},{72,80},{88,96},{104,112},{120,128}... | collective-permute-start | bytes 1179656 | tf_op jit(solution)/shard_map/ppermute | solution.py:459
  23.2 26.7 %copy-start.1 = (f32[16,3,2,16,128]{4,3,2,1,0:T(8,128)S(1)}, f32[16,3,2,16,128]{4,3,2,1,0:T(8,128)}, u32[]{:S(2)}) copy-start(f32[16,3,2,16,128]{4,3,2,1,0:T(8,128)} %param.5) | copy-start | bytes 2359300
  23.3 18.8 %collective-permute-start.9 = (f32[2,3,2,16,128]{4,3,2,1,0:T(8,128)S(1)}, f32[2,3,2,16,128]{4,3,2,1,0:T(8,128)S(1)}, u32[]{:S(2)}, u32[]{:S(2)}) collective-permute-start(f32[2,3,2,16,128]{4,3,2,1,0:T(8,128)S(1)} %get-tuple-element.35), channel_id=1, source_target_pairs={{0,5},{1,6},{2,7},{3,0},{4,1},{5,2},{6,3},{7,4},{8,13},{9,14},{10,... | collective-permute-start | bytes 294920 | tf_op jit(solution)/shard_map/ppermute | solution.py:434
  30.1 11.3 %collective-permute-start.7 = (f32[1,3,2,16,128]{4,3,2,1,0:T(8,128)S(1)}, f32[1,3,2,16,128]{4,3,2,1,0:T(8,128)S(1)}, u32[]{:S(2)}, u32[]{:S(2)}) collective-permute-start(f32[1,3,2,16,128]{4,3,2,1,0:T(8,128)S(1)} %get-tuple-element.40), channel_id=1, source_target_pairs={{0,6},{1,7},{2,0},{3,1},{4,2},{5,3},{6,4},{7,5},{8,14},{9,15},{10,... | collective-permute-start | bytes 147464 | tf_op jit(solution)/shard_map/ppermute | solution.py:434
  30.7 10.7 %collective-permute-start.6 = (f32[1,3,2,16,128]{4,3,2,1,0:T(8,128)S(1)}, f32[1,3,2,16,128]{4,3,2,1,0:T(8,128)S(1)}, u32[]{:S(2)}, u32[]{:S(2)}) collective-permute-start(f32[1,3,2,16,128]{4,3,2,1,0:T(8,128)S(1)} %get-tuple-element.41), channel_id=1, source_target_pairs={{0,4},{1,5},{2,6},{3,7},{4,0},{5,1},{6,2},{7,3},{8,12},{9,13},{10,... | collective-permute-start | bytes 147464 | tf_op jit(solution)/shard_map/ppermute | solution.py:434
  35.2 14.1 %collective-permute-start.10 = (f32[2,3,2,16,128]{4,3,2,1,0:T(8,128)S(1)}, f32[2,3,2,16,128]{4,3,2,1,0:T(8,128)S(1)}, u32[]{:S(2)}, u32[]{:S(2)}) collective-permute-start(f32[2,3,2,16,128]{4,3,2,1,0:T(8,128)S(1)} %get-tuple-element.34), channel_id=1, source_target_pairs={{0,6},{1,7},{2,0},{3,1},{4,2},{5,3},{6,4},{7,5},{8,14},{9,15},{10,... | collective-permute-start | bytes 294920 | tf_op jit(solution)/shard_map/ppermute | solution.py:434
  36.7 14.9 %collective-permute-start.11 = (f32[2,3,2,16,128]{4,3,2,1,0:T(8,128)S(1)}, f32[2,3,2,16,128]{4,3,2,1,0:T(8,128)S(1)}, u32[]{:S(2)}, u32[]{:S(2)}) collective-permute-start(f32[2,3,2,16,128]{4,3,2,1,0:T(8,128)S(1)} %get-tuple-element.33), channel_id=1, source_target_pairs={{0,7},{1,0},{2,1},{3,2},{4,3},{5,4},{6,5},{7,6},{8,15},{9,8},{10,9... | collective-permute-start | bytes 294920 | tf_op jit(solution)/shard_map/ppermute | solution.py:434
  41.4 10.1 %collective-permute-start.3 = (f32[2,3,2,16,128]{4,3,2,1,0:T(8,128)S(1)}, f32[2,3,2,16,128]{4,3,2,1,0:T(8,128)S(1)}, u32[]{:S(2)}, u32[]{:S(2)}) collective-permute-start(f32[2,3,2,16,128]{4,3,2,1,0:T(8,128)S(1)} %get-tuple-element.38), channel_id=1, source_target_pairs={{0,1},{1,2},{2,3},{3,4},{4,5},{5,6},{6,7},{7,0},{8,9},{9,10},{10,1... | collective-permute-start | bytes 294920 | tf_op jit(solution)/shard_map/ppermute | solution.py:434
  41.4 10.1 %collective-permute-start.4 = (f32[2,3,2,16,128]{4,3,2,1,0:T(8,128)S(1)}, f32[2,3,2,16,128]{4,3,2,1,0:T(8,128)S(1)}, u32[]{:S(2)}, u32[]{:S(2)}) collective-permute-start(f32[2,3,2,16,128]{4,3,2,1,0:T(8,128)S(1)} %get-tuple-element.37), channel_id=1, source_target_pairs={{0,2},{1,3},{2,4},{3,5},{4,6},{5,7},{6,0},{7,1},{8,10},{9,11},{10,... | collective-permute-start | bytes 294920 | tf_op jit(solution)/shard_map/ppermute | solution.py:434
  42.1 14.3 %collective-permute-start.5 = (f32[2,3,2,16,128]{4,3,2,1,0:T(8,128)S(1)}, f32[2,3,2,16,128]{4,3,2,1,0:T(8,128)S(1)}, u32[]{:S(2)}, u32[]{:S(2)}) collective-permute-start(f32[2,3,2,16,128]{4,3,2,1,0:T(8,128)S(1)} %get-tuple-element.36), channel_id=1, source_target_pairs={{0,3},{1,4},{2,5},{3,6},{4,7},{5,0},{6,1},{7,2},{8,11},{9,12},{10,... | collective-permute-start | bytes 294920 | tf_op jit(solution)/shard_map/ppermute | solution.py:434
  49.3 7.0 %collective-permute-start.8 = (f32[1,3,2,16,128]{4,3,2,1,0:T(8,128)S(1)}, f32[1,3,2,16,128]{4,3,2,1,0:T(8,128)S(1)}, u32[]{:S(2)}, u32[]{:S(2)}) collective-permute-start(f32[1,3,2,16,128]{4,3,2,1,0:T(8,128)S(1)} %collective-permute-done.7), channel_id=1, source_target_pairs={{0,6},{1,7},{2,0},{3,1},{4,2},{5,3},{6,4},{7,5},{8,14},{9,15},{10,... | collective-permute-start | bytes 147464 | tf_op jit(solution)/shard_map/ppermute | solution.py:434
  88.6 14.3 %collective-permute-start.12 = (f32[2,3,2,16,128]{4,3,2,1,0:T(8,128)S(1)}, f32[2,3,2,16,128]{4,3,2,1,0:T(8,128)S(1)}, u32[]{:S(2)}, u32[]{:S(2)}) collective-permute-start(f32[2,3,2,16,128]{4,3,2,1,0:T(8,128)S(1)} %bitcast.53), channel_id=1, source_target_pairs={{0,1},{1,2},{2,3},{3,4},{4,5},{5,6},{6,7},{7,0},{8,9},{9,10},{10,1... | collective-permute-start | bytes 294920 | tf_op jit(solution)/shard_map/ppermute | solution.py:434
  89.3 10.1 %collective-permute-start.16 = (f32[1,3,2,16,128]{4,3,2,1,0:T(8,128)S(1)}, f32[1,3,2,16,128]{4,3,2,1,0:T(8,128)S(1)}, u32[]{:S(2)}, u32[]{:S(2)}) collective-permute-start(f32[1,3,2,16,128]{4,3,2,1,0:T(8,128)S(1)} %bitcast.55), channel_id=1, source_target_pairs={{0,6},{1,7},{2,0},{3,1},{4,2},{5,3},{6,4},{7,5},{8,14},{9,15},{10,... | collective-permute-start | bytes 147464 | tf_op jit(solution)/shard_map/ppermute | solution.py:434
  90.7 8.7 %collective-permute-start.15 = (f32[1,3,2,16,128]{4,3,2,1,0:T(8,128)S(1)}, f32[1,3,2,16,128]{4,3,2,1,0:T(8,128)S(1)}, u32[]{:S(2)}, u32[]{:S(2)}) collective-permute-start(f32[1,3,2,16,128]{4,3,2,1,0:T(8,128)S(1)} %bitcast.54), channel_id=1, source_target_pairs={{0,4},{1,5},{2,6},{3,7},{4,0},{5,1},{6,2},{7,3},{8,12},{9,13},{10,... | collective-permute-start | bytes 147464 | tf_op jit(solution)/shard_map/ppermute | solution.py:434
  93.7 12.9 %collective-permute-start.13 = (f32[2,3,2,16,128]{4,3,2,1,0:T(8,128)S(1)}, f32[2,3,2,16,128]{4,3,2,1,0:T(8,128)S(1)}, u32[]{:S(2)}, u32[]{:S(2)}) collective-permute-start(f32[2,3,2,16,128]{4,3,2,1,0:T(8,128)S(1)} %bitcast.52), channel_id=1, source_target_pairs={{0,2},{1,3},{2,4},{3,5},{4,6},{5,7},{6,0},{7,1},{8,10},{9,11},{10,... | collective-permute-start | bytes 294920 | tf_op jit(solution)/shard_map/ppermute | solution.py:434
  94.3 13.0 %collective-permute-start.14 = (f32[2,3,2,16,128]{4,3,2,1,0:T(8,128)S(1)}, f32[2,3,2,16,128]{4,3,2,1,0:T(8,128)S(1)}, u32[]{:S(2)}, u32[]{:S(2)}) collective-permute-start(f32[2,3,2,16,128]{4,3,2,1,0:T(8,128)S(1)} %bitcast.51), channel_id=1, source_target_pairs={{0,3},{1,4},{2,5},{3,6},{4,7},{5,0},{6,1},{7,2},{8,11},{9,12},{10,... | collective-permute-start | bytes 294920 | tf_op jit(solution)/shard_map/ppermute | solution.py:434
  99.4 10.5 %collective-permute-start.18 = (f32[2,3,2,16,128]{4,3,2,1,0:T(8,128)S(1)}, f32[2,3,2,16,128]{4,3,2,1,0:T(8,128)S(1)}, u32[]{:S(2)}, u32[]{:S(2)}) collective-permute-start(f32[2,3,2,16,128]{4,3,2,1,0:T(8,128)S(1)} %bitcast.50), channel_id=1, source_target_pairs={{0,5},{1,6},{2,7},{3,0},{4,1},{5,2},{6,3},{7,4},{8,13},{9,14},{10,... | collective-permute-start | bytes 294920 | tf_op jit(solution)/shard_map/ppermute | solution.py:434
  99.4 12.8 %collective-permute-start.19 = (f32[2,3,2,16,128]{4,3,2,1,0:T(8,128)S(1)}, f32[2,3,2,16,128]{4,3,2,1,0:T(8,128)S(1)}, u32[]{:S(2)}, u32[]{:S(2)}) collective-permute-start(f32[2,3,2,16,128]{4,3,2,1,0:T(8,128)S(1)} %bitcast.49), channel_id=1, source_target_pairs={{0,6},{1,7},{2,0},{3,1},{4,2},{5,3},{6,4},{7,5},{8,14},{9,15},{10,... | collective-permute-start | bytes 294920 | tf_op jit(solution)/shard_map/ppermute | solution.py:434
  102.9 10.2 %collective-permute-start.20 = (f32[2,3,2,16,128]{4,3,2,1,0:T(8,128)S(1)}, f32[2,3,2,16,128]{4,3,2,1,0:T(8,128)S(1)}, u32[]{:S(2)}, u32[]{:S(2)}) collective-permute-start(f32[2,3,2,16,128]{4,3,2,1,0:T(8,128)S(1)} %bitcast.48), channel_id=1, source_target_pairs={{0,7},{1,0},{2,1},{3,2},{4,3},{5,4},{6,5},{7,6},{8,15},{9,8},{10,9... | collective-permute-start | bytes 294920 | tf_op jit(solution)/shard_map/ppermute | solution.py:434
  106.6 8.3 %collective-permute-start.17 = (f32[1,3,2,16,128]{4,3,2,1,0:T(8,128)S(1)}, f32[1,3,2,16,128]{4,3,2,1,0:T(8,128)S(1)}, u32[]{:S(2)}, u32[]{:S(2)}) collective-permute-start(f32[1,3,2,16,128]{4,3,2,1,0:T(8,128)S(1)} %collective-permute-done.16), channel_id=1, source_target_pairs={{0,6},{1,7},{2,0},{3,1},{4,2},{5,3},{6,4},{7,5},{8,14},{9,15},{10,... | collective-permute-start | bytes 147464 | tf_op jit(solution)/shard_map/ppermute | solution.py:434
